TPU v7x, 32 devices: a whole 2x2x4 slice. The times are simulated.
32 devices in a mesh: angle: 2 (over y), row: 8 (over z, x), col: 2 (over core).
Axes of the slice: x: 2, y: 2, z: 4, core: 2. Of those that a mesh axis runs over, the one named last changes fastest.
Arguments:
- obj_field: float32 [2, 2048, 1024], P(None, ('angle', 'row'), 'col'), parts along dimension 1, may hold values from -6 to 6
- probe_modes: bfloat16 [2, 6, 256, 256], replicated, may hold values from -6 to 6
- centers: int32 [32, 2], P(('angle', 'row', 'col')), parts along dimension 0, may hold values from 0 to 1023, as said below
- amplitudes: float32 [32, 256, 256], P(('angle', 'row', 'col')), parts along dimension 0, may hold values from 0.2 to 4
Outputs:
- new_object: float32 [2, 2048, 1024], P(None, ('angle', 'row'), 'col'), parts along dimension 1
- new_probe: float32 [2, 12, 256, 256], P(None, 'angle'), parts along dimension 1
There are 2 independent parts, one for each index of `angle`. A program takes and returns all parts, laid end to end along the dimension named above; an argument that names none is the same for every part. Nothing has to cross between parts.
Inputs may be any that keep to these rules, and one draw needn't show every extreme that they name: `centers`: position k belongs to device d = k // 1 of the row+col order (row slowest); its centre lies in that device's tile: row in [(d // (1024 // 512)) * 128, + 128), column in [(d % (1024 // 512)) * 512, + 512).
All inputs are finite; a program needn't handle non-finite values.
Results may differ from a plain program's by a relative error of at most 0.0003.
Values sent between devices are 32-bit elements; how exact they have to be, the bound alone decides.
A program may use at most 64 MiB of HBM per device.

v0:
```python
import functools
import math

import jax
import jax.numpy as jnp
import numpy as np
from jax import lax
from jax.experimental import pallas as pl
from jax.experimental.pallas import tpu as pltpu
from jax.sharding import PartitionSpec as P

MESH = pl.DeviceIdType.MESH
F32 = jnp.float32
BF16 = jnp.bfloat16
VMEM = pl.BlockSpec(memory_space=pltpu.VMEM)
SMEM = pl.BlockSpec(memory_space=pltpu.SMEM)
LIMIT = 60 * 1024 * 1024


def padded(block, sides, width):
    for axis, dim in sides:
        count = lax.axis_size(axis)
        forward = [(i, i + 1) for i in range(count - 1)]
        backward = [(target, source) for source, target in forward]
        low = lax.ppermute(
            lax.slice_in_dim(block, block.shape[dim] - width, None, axis=dim), axis, forward
        )
        high = lax.ppermute(lax.slice_in_dim(block, 0, width, axis=dim), axis, backward)
        block = jnp.concatenate([low, block, high], axis=dim)
    return block


def split(x):
    high = x.astype(BF16)
    return high, (x - high.astype(F32)).astype(BF16)


def dot(a, b):
    return jnp.dot(a, b, preferred_element_type=F32)


def dot3(a, b):
    return dot(a[0], b[1]) + dot(a[1], b[0]) + dot(a[0], b[0])


def tables(side):
    half = side // 2
    k = np.arange(half)
    phase = (k[:, None] * k[None, :] % half) * (2.0 * math.pi / half)
    scale = 1.0 / math.sqrt(side)
    cosine, sine = np.cos(phase) * scale, np.sin(phase) * scale
    matrix = np.block([[cosine, sine], [-sine, cosine]]).astype(np.float32)
    turn = k * (2.0 * math.pi / side)
    lanes = np.stack([np.cos(turn), np.sin(turn)]).astype(np.float32)
    rows = np.broadcast_to(lanes[:, :, None], (2, half, side))
    order = np.concatenate([np.arange(0, side, 2), np.arange(1, side, 2)])
    shuffle = (np.arange(side)[:, None] == order[None, :]).astype(np.float32)
    high = matrix.astype(BF16)
    low = (matrix - high.astype(np.float32)).astype(BF16)
    return (
        jnp.asarray(np.stack([high, low])),
        jnp.asarray(np.stack([high.T, low.T])),
        jnp.asarray(rows),
        jnp.asarray(lanes),
        jnp.asarray(np.stack([shuffle, shuffle.T])).astype(BF16),
    )


def cat(parts, axis):
    return jnp.concatenate(parts, axis=axis)


def forward_transform(re, im, a, b, rows, lanes):
    h = re.shape[0] // 2
    n = 2 * h
    er, ei = re[:h] + re[h:], im[:h] + im[h:]
    dr, di = re[:h] - re[h:], im[:h] - im[h:]
    c, s = rows
    stacked = cat([cat([er, dr * c + di * s], 1), cat([ei, di * c - dr * s], 1)], 0)
    y = dot3(a, split(stacked))
    yr = cat([y[:h, :n], y[:h, n:]], 0)
    yi = cat([y[h:, :n], y[h:, n:]], 0)
    er, ei = yr[:, :h] + yr[:, h:], yi[:, :h] + yi[:, h:]
    dr, di = yr[:, :h] - yr[:, h:], yi[:, :h] - yi[:, h:]
    c, s = lanes
    stacked = cat([cat([er, ei], 1), cat([dr * c + di * s, di * c - dr * s], 1)], 0)
    z = dot3(split(stacked), b)
    return cat([z[:n, :h], z[n:, :h]], 1), cat([z[:n, h:], z[n:, h:]], 1)


def inverse_transform(fr, fi, a, b, rows, lanes):
    h = fr.shape[0] // 2
    n = 2 * h
    stacked = cat([cat([fr[:, :h], fi[:, :h]], 1), cat([fr[:, h:], fi[:, h:]], 1)], 0)
    z = dot3(split(stacked), a)
    er, ei, odr, odi = z[:n, :h], z[:n, h:], z[n:, :h], z[n:, h:]
    c, s = lanes
    tr, ti = odr * c - odi * s, odi * c + odr * s
    yr = cat([er + tr, er - tr], 1)
    yi = cat([ei + ti, ei - ti], 1)
    stacked = cat([cat([yr[:h], yr[h:]], 1), cat([yi[:h], yi[h:]], 1)], 0)
    v = dot3(b, split(stacked))
    er, ei, odr, odi = v[:h, :n], v[h:, :n], v[:h, n:], v[h:, n:]
    c, s = rows
    tr, ti = odr * c - odi * s, odi * c + odr * s
    return cat([er + tr, er - tr], 0), cat([ei + ti, ei - ti], 0)


def row_picker(count, depth, start, valid):
    place = lax.broadcasted_iota(jnp.int32, (count, depth), 0) - lax.broadcasted_iota(
        jnp.int32, (count, depth), 1
    )
    hit = (place == start) & (valid != 0)
    return jnp.where(hit, 1.0, 0.0).astype(BF16)


def col_picker(depth, count, start):
    place = lax.broadcasted_iota(jnp.int32, (depth, count), 1) - lax.broadcasted_iota(
        jnp.int32, (depth, count), 0
    )
    return jnp.where(place == start, 1.0, 0.0).astype(BF16)


def update_kernel(
    places, window, probe, amp, a_ref, b_ref, rows_ref, lanes_ref, shuffle,
    grad, numer, illum, peak, far, power,
):
    modes, side = probe.shape[1], probe.shape[2]
    half = side // 2
    a = (a_ref[0], a_ref[1])
    b = (b_ref[0], b_ref[1])
    rows = (rows_ref[0], rows_ref[1])
    lanes = (lanes_ref[0:1, :], lanes_ref[1:2, :])

    def wave(m):
        pr, pi = probe[0, m].astype(F32), probe[1, m].astype(F32)
        wr, wi = window[0], window[1]
        return pr, pi, wr, wi, pr * wr - pi * wi, pr * wi + pi * wr

    power[...] = jnp.zeros_like(power)

    def ahead(m, carry):
        pr, pi, wr, wi, xr, xi = wave(m)
        fr, fi = forward_transform(xr, xi, a, b, rows, lanes)
        far[0, m] = fr
        far[1, m] = fi
        power[0] += fr * fr + fi * fi
        power[1] += pr * pr + pi * pi
        return carry

    lax.fori_loop(0, modes, ahead, 0)
    measured = 0.0
    rest = amp[...]
    for i in range(3):
        piece = rest.astype(BF16)
        rest = rest - piece.astype(F32)
        measured += dot(dot(shuffle[1], piece).astype(BF16), shuffle[0])
    power[0] = measured / (jnp.sqrt(power[0]) + 0.5)
    high, low = split(power[1])
    tile_rows, tile_cols = illum.shape
    spot = cat([high, low], 1)
    illum[...] = jnp.zeros_like(illum)

    def place_spot(k, carry):
        picked = dot(row_picker(tile_rows, side, places[k, 0], places[k, 2]), spot).astype(BF16)
        across = col_picker(side, tile_cols, places[k, 1])
        placed = dot(cat([picked[:, :side], picked[:, side:]], 0), across)
        illum[...] += placed[:tile_rows] + placed[tile_rows:]
        return carry

    lax.fori_loop(0, places.shape[0], place_spot, 0)
    peak[...] = jnp.full(peak.shape, jnp.max(illum[...]), F32)
    numer[...] = jnp.zeros_like(numer)

    def back(m, carry):
        pr, pi, wr, wi, xr, xi = wave(m)
        factor = power[0]
        gr, gi = inverse_transform(far[0, m] * factor, far[1, m] * factor, a, b, rows, lanes)
        dr, di = gr - xr, gi - xi
        numer[0] += pr * dr + pi * di
        numer[1] += pr * di - pi * dr
        ur = wr * dr + wi * di
        ui = wr * di - wi * dr
        for t in range(2):
            grad[t, pl.ds(pl.multiple_of(m * half, half), half), :] = ur[t * half : (t + 1) * half]
            grad[t, pl.ds(pl.multiple_of((modes + m) * half, half), half), :] = ui[
                t * half : (t + 1) * half
            ]
        return carry

    lax.fori_loop(0, modes, back, 0)
    weight = window[0] * window[0] + window[1] * window[1]
    top = 2 * modes * half
    for t in range(2):
        grad[t, top : top + half, :] = weight[t * half : (t + 1) * half]
        if grad.shape[1] > top + half:
            grad[t, top + half :, :] = jnp.zeros((grad.shape[1] - top - half, side), F32)


def ring_split(lines, ring):
    chunk = -(-lines // (16 * ring)) * 8
    pieces = min(4, chunk // 8)
    offsets, at = [], 0
    for i in range(pieces):
        size = (chunk // 8 // pieces + (1 if i < chunk // 8 % pieces else 0)) * 8
        offsets.append((at, size))
        at += size
    return chunk, offsets


def exchange_kernel(
    ring, chunk, pieces, grad, numer, peak, total, rims, mate, top,
    own, inbox, other, peaks, core_s, core_r, rs_s, rs_r, ag_s, ag_r, dd_s, dd_r,
    rim_s, rim_r, fwd_s, fwd_r, pk_s, pk_r,
):
    row, col = lax.axis_index("row"), lax.axis_index("col")
    side = grad.shape[2]
    half = side // 2
    mine = col
    odd = lax.rem(row, 2)
    at = jnp.where(odd == 1, ring - 1 - row // 2, row // 2)

    def row_at(p):
        p = lax.rem(p + ring, ring)
        return jnp.where(p < ring // 2, 2 * p, 2 * (ring - 1 - p) + 1)

    targets = (row_at(at + 1), row_at(at - 1))
    place = (at, lax.rem(ring - at, ring))
    has_up, has_down = row > 0, row < ring - 1

    barrier = pltpu.get_barrier_semaphore()

    def greet(r, c):
        pl.semaphore_signal(
            barrier, inc=1, device_id={"row": r, "col": c}, device_id_type=MESH
        )

    greet(row, 1 - col)
    greet(targets[0], col)
    greet(targets[1], col)

    @pl.when(has_up)
    def _():
        greet(row - 1, col)

    @pl.when(has_down)
    def _():
        greet(row + 1, col)

    pl.semaphore_wait(barrier, 3 + jnp.where(has_up, 1, 0) + jnp.where(has_down, 1, 0))

    def remote(src, dst, s, r, to_row, to_col):
        return pltpu.make_async_remote_copy(
            src_ref=src, dst_ref=dst, send_sem=s, recv_sem=r,
            device_id={"row": to_row, "col": to_col}, device_id_type=MESH,
        )

    first = remote(grad.at[1 - mine], other, core_s.at[0], core_r.at[0], row, 1 - col)
    first.start()
    peak_first = remote(peak, peaks.at[0], pk_s.at[0], pk_r.at[0], row, 1 - col)
    peak_first.start()
    numer_copy = remote(numer, mate, core_s.at[1], core_r.at[1], row, 1 - col)
    numer_copy.start()
    up = remote(
        numer.at[:, pl.ds(0, half), :], rims.at[mine, 1], rim_s.at[0], rim_r.at[1],
        row - 1, col,
    )
    down = remote(
        numer.at[:, pl.ds(half, half), :], rims.at[mine, 0], rim_s.at[1], rim_r.at[0],
        row + 1, col,
    )

    @pl.when(has_up)
    def _():
        up.start()

    @pl.when(has_down)
    def _():
        down.start()

    def spot(k, d, u):
        k = lax.rem(k + 2 * ring, ring)
        start = (k * 2 + d) * chunk + pieces[u][0]
        return pl.ds(pl.multiple_of(start, 8), pieces[u][1])

    def box(d, u):
        return pl.ds(d * chunk + pieces[u][0], pieces[u][1])

    streams = [(d, u) for u in range(len(pieces)) for d in range(2)]

    def rs_copy(src, s, d, u):
        return remote(
            src, inbox.at[s, box(d, u), :], rs_s.at[s, d, u], rs_r.at[s, d, u], targets[d], col
        )

    def ag_copy(s, d, u):
        here = total.at[mine, spot(place[d] + 1 - s, d, u), :]
        return remote(here, here, ag_s.at[s, d, u], ag_r.at[s, d, u], targets[d], col)

    def dd_copy(s, d, u):
        here = total.at[mine, spot(place[d] + 1 - s, d, u), :]
        return remote(here, here, dd_s.at[s, d, u], dd_r.at[s, d, u], row, 1 - col)

    def pk_copy(src, s):
        return remote(src, peaks.at[s + 1], pk_s.at[s + 1], pk_r.at[s + 1], targets[0], col)

    peak_first.wait()
    top[...] = jnp.maximum(peak[...], peaks[0])
    pk_copy(top, 0).start()
    first.wait()
    own[...] = grad[mine] + other[...]
    for d, u in streams:
        rs_copy(own.at[spot(place[d], d, u), :], 0, d, u).start()

    def scatter_step(s, carry):
        pk_copy(top, s).wait_recv()
        peaks[s + 1] = jnp.maximum(peaks[s + 1], top[...])
        pk_copy(peaks.at[s + 1], s + 1).start()
        for d, u in streams:
            rs_copy(own.at[spot(0, d, u), :], s, d, u).wait_recv()
            inbox[s, box(d, u), :] += own[spot(place[d] - s - 1, d, u), :]
            rs_copy(inbox.at[s, box(d, u), :], s + 1, d, u).start()
        return carry

    lax.fori_loop(0, ring - 2, scatter_step, 0)
    last = ring - 2
    for d, u in streams:
        rs_copy(own.at[spot(0, d, u), :], last, d, u).wait_recv()
        here = spot(place[d] + 1, d, u)
        total[mine, here, :] = inbox[last, box(d, u), :] + own[here, :]
        ag_copy(0, d, u).start()
        dd_copy(0, d, u).start()
    pk_copy(top, last).wait_recv()

    fwd = [
        remote(rims.at[mine, t], rims.at[mine, t], fwd_s.at[t], fwd_r.at[t], row, 1 - col)
        for t in range(2)
    ]

    @pl.when(has_down)
    def _():
        remote(
            numer.at[:, pl.ds(0, half), :], rims.at[mine, 1], rim_s.at[0], rim_r.at[1],
            row + 1, col,
        ).wait_recv()
        fwd[1].start()

    @pl.when(has_up)
    def _():
        remote(
            numer.at[:, pl.ds(half, half), :], rims.at[mine, 0], rim_s.at[1], rim_r.at[0],
            row - 1, col,
        ).wait_recv()
        fwd[0].start()

    def gather_step(s, carry):
        for d, u in streams:
            ag_copy(s, d, u).wait_recv()

            @pl.when(s < ring - 2)
            def _():
                ag_copy(s + 1, d, u).start()

            dd_copy(s + 1, d, u).start()
        return carry

    lax.fori_loop(0, ring - 1, gather_step, 0)

    def finish(s, carry):
        for d, u in streams:
            rs_copy(own.at[spot(0, d, u), :], s, d, u).wait_send()
            ag_copy(s, d, u).wait_send()
            dd_copy(s, d, u).wait()
        pk_copy(top, s).wait_send()
        return carry

    lax.fori_loop(0, ring - 1, finish, 0)
    for d, u in streams:
        dd_copy(ring - 1, d, u).wait()
    numer_copy.wait()

    @pl.when(has_up)
    def _():
        up.wait_send()
        fwd[0].wait()

    @pl.when(has_down)
    def _():
        down.wait_send()
        fwd[1].wait()

    top[...] = jnp.maximum(peaks[ring - 1], top[...])


def object_kernel(places, here, obj, numer, mate, rims, illum, top, out, acc):
    tile_rows, tile_cols = illum.shape
    side = numer.shape[2]
    half = side // 2
    mine = here[0]
    acc[...] = jnp.zeros_like(acc)

    def put(block, start, k):
        valid = places[k, 2]
        block = jnp.where(valid != 0, block, 0.0)
        rh, rl = split(block[0])
        ih, il = split(block[1])
        stacked = cat([rh, ih, rl, il], 1)
        picked = dot(row_picker(tile_rows, block.shape[1], start, valid), stacked).astype(BF16)
        tall = cat([picked[:, i * side : (i + 1) * side] for i in range(4)], 0)
        acc[...] += dot(tall, col_picker(side, tile_cols, places[k, 1]))

    for c in range(2):
        put(jnp.where(mine == c, numer[...], mate[...]), places[2 + c, 0], 2 + c)
        put(rims[c, 0], places[c, 0] + half, c)
        put(rims[c, 1], places[4 + c, 0], 4 + c)
    scale = 1.0 / (illum[...] + 0.1 * jnp.max(top[...]))
    for t in range(2):
        high = acc[t * tile_rows : (t + 1) * tile_rows]
        low = acc[(2 + t) * tile_rows : (3 + t) * tile_rows]
        out[t] = obj[t] + (high + low) * scale


def probe_kernel(probe, total, out):
    modes, side = probe.shape[1], probe.shape[2]
    half = side // 2
    top = 2 * modes * half
    biggest = jnp.max(
        jnp.maximum(total[0, top : top + half, :], total[1, top : top + half, :])
    )
    for t in range(2):
        scale = 1.0 / (total[t, top : top + half, :] + 0.1 * biggest)
        for i in range(2):
            for m in range(modes):
                line = (i * modes + m) * half
                out[i, m, t * half : (t + 1) * half, :] = (
                    probe[i, m, t * half : (t + 1) * half, :].astype(F32)
                    + total[t, line : line + half, :] * scale
                )


def struct(shape, kind=F32):
    return jax.ShapeDtypeStruct(shape, kind)


def local(obj_field, probe_modes, centers, amplitudes):
    tile_rows, tile_cols = obj_field.shape[1:]
    modes, side = probe_modes.shape[1:3]
    margin = side // 2
    ring, cores = lax.axis_size("row"), lax.axis_size("col")
    row, col = lax.axis_index("row"), lax.axis_index("col")
    origin = jnp.stack([row * tile_rows, col * tile_cols]).astype(jnp.int32)

    extended = padded(obj_field, (("row", 1), ("col", 2)), margin)
    near = padded(centers.reshape(1, 1, 2), (("row", 0),), 1)
    mate_list = lax.ppermute(near, "col", [(0, 1), (1, 0)])
    listed = jnp.where(
        col == 0, jnp.concatenate([near, mate_list], 1), jnp.concatenate([mate_list, near], 1)
    ).reshape(3 * cores, 2)
    steps = jnp.arange(3 * cores, dtype=jnp.int32) // cores - 1 + row
    valid = ((steps >= 0) & (steps < ring)).astype(jnp.int32)
    places = jnp.concatenate([listed - margin - origin, valid[:, None]], 1)
    start = centers[0] - origin
    window = lax.dynamic_slice(extended, (0, start[0], start[1]), (2, side, side))

    lines = (2 * modes + 1) * margin
    chunk, pieces = ring_split(lines, ring)
    depth = 2 * ring * chunk
    count = len(pieces)
    params = pltpu.CompilerParams(vmem_limit_bytes=LIMIT)
    grad, numer, illum, peak = pl.pallas_call(
        update_kernel,
        out_shape=(
            struct((2, depth, side)),
            struct((2, side, side)),
            struct((tile_rows, tile_cols)),
            struct((8, 128)),
        ),
        in_specs=[SMEM] + [VMEM] * 8,
        out_specs=(VMEM,) * 4,
        scratch_shapes=[
            pltpu.VMEM((2, modes, side, side), F32),
            pltpu.VMEM((2, side, side), F32),
        ],
        compiler_params=params,
        name="update",
    )(places, window, probe_modes, amplitudes[0], *tables(side))

    dma = pltpu.SemaphoreType.DMA
    total, rims, mate, top = pl.pallas_call(
        functools.partial(exchange_kernel, ring, chunk, pieces),
        out_shape=(
            struct((2, depth, side)),
            struct((2, 2, 2, margin, side)),
            struct((2, side, side)),
            struct((8, 128)),
        ),
        in_specs=[VMEM] * 3,
        out_specs=(VMEM,) * 4,
        scratch_shapes=[
            pltpu.VMEM((depth, side), F32),
            pltpu.VMEM((ring - 1, 2 * chunk, side), F32),
            pltpu.VMEM((depth, side), F32),
            pltpu.VMEM((ring, 8, 128), F32),
            dma((2,)), dma((2,)),
            dma((ring - 1, 2, count)), dma((ring - 1, 2, count)),
            dma((ring - 1, 2, count)), dma((ring - 1, 2, count)),
            dma((ring, 2, count)), dma((ring, 2, count)),
            dma((2,)), dma((2,)), dma((2,)), dma((2,)),
            dma((ring,)), dma((ring,)),
        ],
        compiler_params=pltpu.CompilerParams(
            vmem_limit_bytes=LIMIT, collective_id=1, has_side_effects=True
        ),
        name="exchange",
    )(grad, numer, peak)

    new_object = pl.pallas_call(
        object_kernel,
        out_shape=struct(obj_field.shape),
        in_specs=[SMEM, SMEM] + [VMEM] * 6,
        out_specs=VMEM,
        scratch_shapes=[pltpu.VMEM((4 * tile_rows, tile_cols), F32)],
        compiler_params=params,
        name="object",
    )(places, col.reshape(1).astype(jnp.int32), obj_field, numer, mate, rims, illum, top)
    new_probe = pl.pallas_call(
        probe_kernel,
        out_shape=struct(probe_modes.shape),
        in_specs=[VMEM] * 2,
        out_specs=VMEM,
        compiler_params=params,
        name="probe",
    )(probe_modes, total)
    return (new_object, new_probe)


def solution(mesh):
    in_specs = (
        P(None, ("angle", "row"), "col"),
        P(),
        P(("angle", "row", "col"), None),
        P(("angle", "row", "col"), None, None),
    )
    out_specs = (P(None, ("angle", "row"), "col"), P(None, "angle", None, None))
    return jax.shard_map(local, mesh=mesh, in_specs=in_specs, out_specs=out_specs, check_vma=False)
```

profile of v0, /device:TPU:0, one launch (start us, length us, event | category | flops | bytes accessed | tf_op | source)
XLA Modules:
  0.0 140.7 jit_solution(16066418058755273427)
XLA Ops:
  0.6 0.7 copy.15
  1.4 1.3 collective-permute-start.1
  2.7 5.5 %collective-permute-start = (s32[1,1,2]{0,2,1:T(2,128)S(1)}, s32[1,1,2]{0,2,1:T(2,128)S(1)}, u32[]{:S(2)}, u32[]{:S(2)}) collective-permute-start(s32[1,1,2]{0,2,1:T(2,128)S(1)} %copy.15), channel_id=1, source_target_pairs={{0,2},{2,4},{4,6},{6,8},{8,10},{10,12},{12,14},{1,3},{3,5},{5,7},{... | collective-permute-start | bytes 32 | tf_op jit(solution)/shard_map/ppermute | solution.py:25
  8.2 1.3 collective-permute-start.4
  9.5 5.5 %collective-permute-start.3 = (f32[2,128,512]{2,1,0:T(8,128)}, f32[2,128,512]{2,1,0:T(8,128)S(1)}, u32[]{:S(2)}, u32[]{:S(2)}) collective-permute-start(f32[2,128,512]{2,1,0:T(8,128)} %obj.1), channel_id=1, source_target_pairs={{0,2},{2,4},{4,6},{6,8},{8,10},{10,12},{12,14},{1,3},{3,5},{5,7},{... | collective-permute-start | bytes 1572872 | tf_op jit(solution)/shard_map/ppermute | solution.py:25
  15.0 0.7 bitcast_subtract_fusion
  15.7 0.6 fusion.13
  20.2 0.1 pad_add_fusion.1
  20.3 0.0 collective-permute-start.2
  20.3 15.7 %collective-permute-done.3 = f32[2,128,512]{2,1,0:T(8,128)S(1)} collective-permute-done((f32[2,128,512]{2,1,0:T(8,128)}, f32[2,128,512]{2,1,0:T(8,128)S(1)}, u32[]{:S(2)}, u32[]{:S(2)}) %collective-permute-start.3) | collective-permute-done | bytes 524320 | tf_op jit(solution)/shard_map/ppermute | solution.py:25
  36.1 1.1 constant_dynamic-update-slice_fusion.1
  37.2 0.1 fusion.12
  37.3 1.3 collective-permute-start.6
  38.6 3.1 %collective-permute-start.5 = (f32[2,384,128]{2,1,0:T(8,128)S(1)}, f32[2,384,128]{2,1,0:T(8,128)S(1)}, u32[]{:S(2)}, u32[]{:S(2)}) collective-permute-start(f32[2,384,128]{2,1,0:T(8,128)S(1)} %get-tuple-element.21), channel_id=1, source_target_pairs={{0,1},{2,3},{4,5},{6,7},{8,9},{10,11},{12,13},{14,15},{16,17},{18,... | collective-permute-start | bytes 1179656 | tf_op jit(solution)/shard_map/ppermute | solution.py:25
  41.7 0.1 fusion.11
  41.8 0.1 copy.20
  41.9 0.7 pad_add_fusion.places
  42.6 0.4 collective-permute-done.5
  43.0 1.2 fusion.1.window
  44.2 0.8 jit_solution_.3.rows_ref
  45.0 20.2 %update.1 = (f32[2,1664,256]{2,1,0:T(8,128)}, f32[2,256,256]{2,1,0:T(8,128)}, f32[128,512]{1,0:T(8,128)}, f32[8,128]{1,0:T(8,128)}) custom-call(s32[6,3]{1,0:T(8,128)} %pad_add_fusion.places, f32[2,256,256]{2,1,0:T(8,128)} %fusion.1.window, bf16[2,6,256,256]{3,2,1,0:T(8,128)(2,1)} %probe.5, f32[256,256]{1,0:T(8,128)} %bitcast.9, ...), custom_call_target="tpu_custom_call" | custom-call | tf_op jit(solution)/shard_map/update/pallas_call | solution.py:470
  65.2 66.5 %exchange.1 = (f32[2,1664,256]{2,1,0:T(8,128)}, f32[2,2,2,128,256]{4,3,2,1,0:T(8,128)}, f32[2,256,256]{2,1,0:T(8,128)}, f32[8,128]{1,0:T(8,128)}) custom-call(f32[2,1664,256]{2,1,0:T(8,128)} %get-tuple-element.11.grad, f32[2,256,256]{2,1,0:T(8,128)} %get-tuple-element.10.numer, f32[8,128]{1,0:T(8,128)} %get-tuple-element.12.peak), custom_call_target="tpu_custom_call" | custom-call | tf_op jit(solution)/shard_map/exchange/pallas_call | solution.py:489
  131.6 4.7 %probe.4 = f32[2,6,256,256]{3,2,1,0:T(8,128)} custom-call(bf16[2,6,256,256]{3,2,1,0:T(8,128)(2,1)} %probe.5, f32[2,1664,256]{2,1,0:T(8,128)} %get-tuple-element.17.total), custom_call_target="tpu_custom_call" | custom-call | tf_op jit(solution)/shard_map/probe/pallas_call | solution.py:526
  136.3 4.4 %object.1 = f32[2,128,512]{2,1,0:T(8,128)} custom-call(s32[6,3]{1,0:T(8,128)} %pad_add_fusion.places, s32[1]{0:T(128)} %bitcast.3.here, f32[2,128,512]{2,1,0:T(8,128)} %obj.1, f32[2,256,256]{2,1,0:T(8,128)} %get-tuple-element.10.numer, f32[2,256,256]{2,1,0:T(8,128)} %get-tuple-element.13.mate, f32[2,2,2,128,256]{4,3,2,1,0:T(8,128)} %get-tuple-element.14.rims, ...), custom_call_target="tpu_custom_call" | custom-call | tf_op jit(solution)/shard_map/object/pallas_call | solution.py:517
  (12 shorter events, 0.1 us)
Async XLA Ops:
  1.4 18.8 %collective-permute-start.1 = (s32[1,1,2]{0,2,1:T(2,128)S(1)}, s32[1,1,2]{0,2,1:T(2,128)S(1)}, u32[]{:S(2)}, u32[]{:S(2)}) collective-permute-start(s32[1,1,2]{0,2,1:T(2,128)S(1)} %copy.15), channel_id=1, source_target_pairs={{2,0},{4,2},{6,4},{8,6},{10,8},{12,10},{14,12},{3,1},{5,3},{7,5},{... | collective-permute-start | bytes 32 | tf_op jit(solution)/shard_map/ppermute | solution.py:28
  2.7 17.5 %collective-permute-start = (s32[1,1,2]{0,2,1:T(2,128)S(1)}, s32[1,1,2]{0,2,1:T(2,128)S(1)}, u32[]{:S(2)}, u32[]{:S(2)}) collective-permute-start(s32[1,1,2]{0,2,1:T(2,128)S(1)} %copy.15), channel_id=1, source_target_pairs={{0,2},{2,4},{4,6},{6,8},{8,10},{10,12},{12,14},{1,3},{3,5},{5,7},{... | collective-permute-start | bytes 32 | tf_op jit(solution)/shard_map/ppermute | solution.py:25
  8.2 29.0 %collective-permute-start.4 = (f32[2,128,512]{2,1,0:T(8,128)}, f32[2,128,512]{2,1,0:T(8,128)S(1)}, u32[]{:S(2)}, u32[]{:S(2)}) collective-permute-start(f32[2,128,512]{2,1,0:T(8,128)} %obj.1), channel_id=1, source_target_pairs={{2,0},{4,2},{6,4},{8,6},{10,8},{12,10},{14,12},{3,1},{5,3},{7,5},{... | collective-permute-start | bytes 1572872 | tf_op jit(solution)/shard_map/ppermute | solution.py:28
  9.5 26.6 %collective-permute-start.3 = (f32[2,128,512]{2,1,0:T(8,128)}, f32[2,128,512]{2,1,0:T(8,128)S(1)}, u32[]{:S(2)}, u32[]{:S(2)}) collective-permute-start(f32[2,128,512]{2,1,0:T(8,128)} %obj.1), channel_id=1, source_target_pairs={{0,2},{2,4},{4,6},{6,8},{8,10},{10,12},{12,14},{1,3},{3,5},{5,7},{... | collective-permute-start | bytes 1572872 | tf_op jit(solution)/shard_map/ppermute | solution.py:25
  20.3 21.4 %collective-permute-start.2 = (s32[3,1,2]{0,2,1:T(2,128)S(1)}, s32[3,1,2]{0,2,1:T(2,128)S(1)}, u32[]{:S(2)}, u32[]{:S(2)}) collective-permute-start(s32[3,1,2]{0,2,1:T(2,128)S(1)} %pad_add_fusion.1), channel_id=1, source_target_pairs={{0,1},{1,0},{2,3},{3,2},{4,5},{5,4},{6,7},{7,6},{8,9},{9,8},{10,11... | collective-permute-start | bytes 80 | tf_op jit(solution)/shard_map/ppermute | solution.py:455
  37.3 6.9 %copy-start = (f32[2,128]{1,0:T(2,128)S(1)}, f32[2,128]{1,0:T(2,128)}, u32[]{:S(2)}) copy-start(f32[2,128]{1,0:T(2,128)} %constant.51.clone.lanes_ref) | copy-start | bytes 3076
  37.3 5.3 %collective-permute-start.6 = (f32[2,384,128]{2,1,0:T(8,128)S(1)}, f32[2,384,128]{2,1,0:T(8,128)S(1)}, u32[]{:S(2)}, u32[]{:S(2)}) collective-permute-start(f32[2,384,128]{2,1,0:T(8,128)S(1)} %get-tuple-element.20), channel_id=1, source_target_pairs={{1,0},{3,2},{5,4},{7,6},{9,8},{11,10},{13,12},{15,14},{17,16},{19,... | collective-permute-start | bytes 1179656 | tf_op jit(solution)/shard_map/ppermute | solution.py:28
  38.6 4.4 %collective-permute-start.5 = (f32[2,384,128]{2,1,0:T(8,128)S(1)}, f32[2,384,128]{2,1,0:T(8,128)S(1)}, u32[]{:S(2)}, u32[]{:S(2)}) collective-permute-start(f32[2,384,128]{2,1,0:T(8,128)S(1)} %get-tuple-element.21), channel_id=1, source_target_pairs={{0,1},{2,3},{4,5},{6,7},{8,9},{10,11},{12,13},{14,15},{16,17},{18,... | collective-permute-start | bytes 1179656 | tf_op jit(solution)/shard_map/ppermute | solution.py:25
where the time goes:
time: 141 us
  Pallas kernels  95.7 us (68%)
  starting transfers between devices  17.9 us (13%)
  waiting for transfers between devices  16.2 us (11%)
  between operations  4.66 us (3%)
  local copies, waits for them, and re-layouts  3.45 us (2%)
  other arithmetic  2.78 us (2%)
    pallas_call x1, Pallas kernels, local(): pl.pallas_call(functools.partial(exchange_kernel, ring, chunk, pieces), o...  66.5 us
    pallas_call x1, Pallas kernels, local(): pl.pallas_call(update_kernel, out_shape=(struct((2, depth, side)), struct...  20.2 us
    ppermute x3, waiting for transfers between devices, padded(): lax.ppermute(lax.slice_in_dim(block, block.shape[dim] - width, None, axis...  16.2 us
    ppermute x3, starting transfers between devices, padded(): lax.ppermute(lax.slice_in_dim(block, block.shape[dim] - width, None, axis...  14.1 us
    pallas_call x1, Pallas kernels, local(): pl.pallas_call(probe_kernel, out_shape=struct(probe_modes.shape), in_spec...  4.69 us
    pallas_call x1, Pallas kernels, local(): pl.pallas_call(object_kernel, out_shape=struct(obj_field.shape), in_specs...  4.41 us
    ppermute x3, starting transfers between devices, padded(): lax.ppermute(lax.slice_in_dim(block, 0, width, axis=dim), axis, backward)  3.86 us
  transfers between devices with their start and end apart: 7, of which 2 were waited for; matrix products, arithmetic and copies ran while one was open for 2% of the time, Pallas kernels for 0%

commit v1 on v0

--- a/solution.py
+++ b/solution.py
@@ -15,19 +15,6 @@
 VMEM = pl.BlockSpec(memory_space=pltpu.VMEM)
 SMEM = pl.BlockSpec(memory_space=pltpu.SMEM)
 LIMIT = 60 * 1024 * 1024
-
-
-def padded(block, sides, width):
-    for axis, dim in sides:
-        count = lax.axis_size(axis)
-        forward = [(i, i + 1) for i in range(count - 1)]
-        backward = [(target, source) for source, target in forward]
-        low = lax.ppermute(
-            lax.slice_in_dim(block, block.shape[dim] - width, None, axis=dim), axis, forward
-        )
-        high = lax.ppermute(lax.slice_in_dim(block, 0, width, axis=dim), axis, backward)
-        block = jnp.concatenate([low, block, high], axis=dim)
-    return block
 
 
 def split(x):
@@ -110,8 +97,7 @@
     place = lax.broadcasted_iota(jnp.int32, (count, depth), 0) - lax.broadcasted_iota(
         jnp.int32, (count, depth), 1
     )
-    hit = (place == start) & (valid != 0)
-    return jnp.where(hit, 1.0, 0.0).astype(BF16)
+    return jnp.where(place == start, valid, 0.0).astype(BF16)
 
 
 def col_picker(depth, count, start):
@@ -121,9 +107,21 @@
     return jnp.where(place == start, 1.0, 0.0).astype(BF16)
 
 
+def corner(known, k, tile_rows, tile_cols, margin):
+    row, col = lax.axis_index("row"), lax.axis_index("col")
+    line = row + k // 2 - 1
+    inside = (line >= 0) & (line < lax.axis_size("row"))
+    mark = known[k]
+    return (
+        mark[0:1, 0:1] - (row * tile_rows + margin),
+        mark[1:2, 0:1] - (col * tile_cols + margin),
+        jnp.where(inside, 1.0, 0.0),
+    )
+
+
 def update_kernel(
-    places, window, probe, amp, a_ref, b_ref, rows_ref, lanes_ref, shuffle,
-    grad, numer, illum, peak, far, power,
+    center, known, column, probe, amp, a_ref, b_ref, rows_ref, lanes_ref, shuffle,
+    grad, numer, illum, peak, far, power, window,
 ):
     modes, side = probe.shape[1], probe.shape[2]
     half = side // 2
@@ -137,6 +135,11 @@
         wr, wi = window[0], window[1]
         return pr, pi, wr, wi, pr * wr - pi * wi, pr * wi + pi * wr
 
+    start = center[0, 0] - lax.axis_index("row") * illum.shape[0]
+    base = pl.multiple_of(start // 8 * 8, 8)
+    shift = lax.rem(side + 8 - lax.rem(start, 8), side + 8)
+    for i in range(2):
+        window[i] = pltpu.roll(column[i, pl.ds(base, side + 8), :], shift, 0)[:side]
     power[...] = jnp.zeros_like(power)
 
     def ahead(m, carry):
@@ -162,13 +165,14 @@
     illum[...] = jnp.zeros_like(illum)
 
     def place_spot(k, carry):
-        picked = dot(row_picker(tile_rows, side, places[k, 0], places[k, 2]), spot).astype(BF16)
-        across = col_picker(side, tile_cols, places[k, 1])
+        top, left, valid = corner(known, k, tile_rows, tile_cols, half)
+        picked = dot(row_picker(tile_rows, side, top, valid), spot).astype(BF16)
+        across = col_picker(side, tile_cols, left)
         placed = dot(cat([picked[:, :side], picked[:, side:]], 0), across)
         illum[...] += placed[:tile_rows] + placed[tile_rows:]
         return carry
 
-    lax.fori_loop(0, places.shape[0], place_spot, 0)
+    lax.fori_loop(0, known.shape[0], place_spot, 0)
     peak[...] = jnp.full(peak.shape, jnp.max(illum[...]), F32)
     numer[...] = jnp.zeros_like(numer)
 
@@ -197,9 +201,131 @@
             grad[t, top + half :, :] = jnp.zeros((grad.shape[1] - top - half, side), F32)
 
 
+def gather_kernel(
+    ring, marks, obj, column, known,
+    strip, packed, near_s, near_r, tile_s, tile_r, pack_s, pack_r, pass_s, pass_r,
+):
+    row, col = lax.axis_index("row"), lax.axis_index("col")
+    tile_rows, tile_cols = obj.shape[1:]
+    side = column.shape[2]
+    half = side // 2
+    has = (row > 0, row < ring - 1)
+    beside = (row - 1, row + 1)
+    barrier = pltpu.get_barrier_semaphore()
+
+    def greet(r, c):
+        pl.semaphore_signal(
+            barrier, inc=1, device_id={"row": r, "col": c}, device_id_type=MESH
+        )
+
+    greet(row, 1 - col)
+    for t in range(2):
+
+        @pl.when(has[t])
+        def _():
+            greet(beside[t], col)
+
+    pl.semaphore_wait(barrier, 1 + jnp.where(has[0], 1, 0) + jnp.where(has[1], 1, 0))
+
+    def remote(src, dst, s, r, to_row, to_col):
+        return pltpu.make_async_remote_copy(
+            src_ref=src, dst_ref=dst, send_sem=s, recv_sem=r,
+            device_id={"row": to_row, "col": to_col}, device_id_type=MESH,
+        )
+
+    def own_lanes(c):
+        return pl.ds(pl.multiple_of(half + c * tile_cols, 128), tile_cols)
+
+    near = [
+        remote(marks, known.at[2 * (1 - t), col], near_s.at[t], near_r.at[1 - t], beside[t], col)
+        for t in range(2)
+    ]
+    mate_mark = remote(marks, known.at[1, col], near_s.at[2], near_r.at[2], row, 1 - col)
+    tile = remote(obj, strip.at[:, :, own_lanes(col)], tile_s, tile_r, row, 1 - col)
+    for t in range(2):
+
+        @pl.when(has[t])
+        def _():
+            near[t].start()
+
+    tile.start()
+    mate_mark.start()
+    strip[:, :, :half] = jnp.zeros((2, tile_rows, half), F32)
+    strip[:, :, half + 2 * tile_cols :] = jnp.zeros((2, tile_rows, half), F32)
+    strip[:, :, own_lanes(col)] = obj[...]
+    tile.wait()
+
+    def cut(mark):
+        width = strip.shape[2]
+        place = lax.broadcasted_iota(jnp.int32, (width, side), 0) - lax.broadcasted_iota(
+            jnp.int32, (width, side), 1
+        )
+        pick = jnp.where(place == mark[1:2, 0:1], 1.0, 0.0).astype(BF16)
+        rest, found = strip[...].reshape(2 * tile_rows, width), 0.0
+        for _ in range(3):
+            piece = rest.astype(BF16)
+            rest = rest - piece.astype(F32)
+            found += dot(piece, pick)
+        return found.reshape(2, tile_rows, side)
+
+    def pack(t):
+        return remote(
+            packed.at[t], column.at[:, pl.ds(2 * (1 - t) * tile_rows, tile_rows), :],
+            pack_s.at[t], pack_r.at[1 - t], beside[t], col,
+        )
+
+    def arrived_pack(t):
+        return remote(
+            packed.at[1 - t], column.at[:, pl.ds(2 * t * tile_rows, tile_rows), :],
+            pack_s.at[1 - t], pack_r.at[t], beside[t], col,
+        )
+
+    def share(t):
+        here = known.at[2 * t, col]
+        return remote(here, here, pass_s.at[t], pass_r.at[t], row, 1 - col)
+
+    for t in range(2):
+
+        @pl.when(has[t])
+        def _():
+            remote(
+                marks, known.at[2 * t, col], near_s.at[1 - t], near_r.at[t], beside[t], col
+            ).wait_recv()
+            share(t).start()
+            packed[t] = cut(known[2 * t, col])
+            pack(t).start()
+
+    known[1, col] = marks[...]
+    column[:, tile_rows : 2 * tile_rows, :] = cut(marks[...])
+    for t in range(2):
+
+        @pl.when(jnp.logical_not(has[t]))
+        def _():
+            column[:, 2 * t * tile_rows : (2 * t + 1) * tile_rows, :] = jnp.zeros(
+                (2, tile_rows, side), F32
+            )
+
+    mate_mark.wait()
+    for t in range(2):
+
+        @pl.when(has[t])
+        def _():
+            share(t).wait()
+
+    for t in range(2):
+
+        @pl.when(has[t])
+        def _():
+            pack(t).wait_send()
+            remote(
+                marks, known.at[2 * (1 - t), col], near_s.at[t], near_r.at[1 - t], beside[t], col
+            ).wait_send()
+            arrived_pack(t).wait_recv()
+
+
 def ring_split(lines, ring):
     chunk = -(-lines // (16 * ring)) * 8
-    pieces = min(4, chunk // 8)
+    pieces = min(2, chunk // 8)
     offsets, at = [], 0
     for i in range(pieces):
         size = (chunk // 8 // pieces + (1 if i < chunk // 8 % pieces else 0)) * 8
@@ -210,8 +336,8 @@
 
 def exchange_kernel(
     ring, chunk, pieces, grad, numer, peak, total, rims, mate, top,
-    own, inbox, other, peaks, core_s, core_r, rs_s, rs_r, ag_s, ag_r, dd_s, dd_r,
-    rim_s, rim_r, fwd_s, fwd_r, pk_s, pk_r,
+    own, inbox, other, seen, highs, core_s, core_r, rs_s, rs_r, ag_s, ag_r, dd_s, dd_r,
+    mine_s, mine_r, rim_s, rim_r, fwd_s, fwd_r, pk_s, pk_r,
 ):
     row, col = lax.axis_index("row"), lax.axis_index("col")
     side = grad.shape[2]
@@ -257,7 +383,7 @@
 
     first = remote(grad.at[1 - mine], other, core_s.at[0], core_r.at[0], row, 1 - col)
     first.start()
-    peak_first = remote(peak, peaks.at[0], pk_s.at[0], pk_r.at[0], row, 1 - col)
+    peak_first = remote(peak, top, core_s.at[2], core_r.at[2], row, 1 - col)
     peak_first.start()
     numer_copy = remote(numer, mate, core_s.at[1], core_r.at[1], row, 1 - col)
     numer_copy.start()
@@ -278,59 +404,97 @@
     def _():
         down.start()
 
-    def spot(k, d, u):
-        k = lax.rem(k + 2 * ring, ring)
-        start = (k * 2 + d) * chunk + pieces[u][0]
+    far = ring // 2
+
+    def reach(b, d):
+        return far if b == d else far - 1
+
+    def spot(q, b, d, u):
+        k = lax.rem(q + 2 * ring, ring)
+        if d == 1:
+            k = lax.rem(ring - k, ring)
+        start = (k * 2 + b) * chunk + pieces[u][0]
         return pl.ds(pl.multiple_of(start, 8), pieces[u][1])
 
-    def box(d, u):
-        return pl.ds(d * chunk + pieces[u][0], pieces[u][1])
-
-    streams = [(d, u) for u in range(len(pieces)) for d in range(2)]
-
-    def rs_copy(src, s, d, u):
+    def box(b, d, u):
+        return pl.ds((2 * b + d) * chunk + pieces[u][0], pieces[u][1])
+
+    flows = [(b, d, u) for u in range(len(pieces)) for b in range(2) for d in range(2)]
+
+    def rs_copy(src, s, b, d, u):
         return remote(
-            src, inbox.at[s, box(d, u), :], rs_s.at[s, d, u], rs_r.at[s, d, u], targets[d], col
-        )
-
-    def ag_copy(s, d, u):
-        here = total.at[mine, spot(place[d] + 1 - s, d, u), :]
-        return remote(here, here, ag_s.at[s, d, u], ag_r.at[s, d, u], targets[d], col)
-
-    def dd_copy(s, d, u):
-        here = total.at[mine, spot(place[d] + 1 - s, d, u), :]
-        return remote(here, here, dd_s.at[s, d, u], dd_r.at[s, d, u], row, 1 - col)
-
-    def pk_copy(src, s):
-        return remote(src, peaks.at[s + 1], pk_s.at[s + 1], pk_r.at[s + 1], targets[0], col)
+            src, inbox.at[s, box(b, d, u), :], rs_s.at[s, b, d, u], rs_r.at[s, b, d, u],
+            targets[d], col,
+        )
+
+    def rs_wait(s, b, d, u):
+        return rs_copy(inbox.at[s, box(b, d, u), :], s, b, d, u)
+
+    def ag_copy(s, b, d, u):
+        here = total.at[mine, spot(place[d] - s, b, d, u), :]
+        return remote(
+            here, here, ag_s.at[s, b, d, u], ag_r.at[s, b, d, u], targets[d], col
+        )
+
+    def dd_copy(s, b, d, u):
+        here = total.at[mine, spot(place[d] - 1 - s, b, d, u), :]
+        return remote(here, here, dd_s.at[s, b, d, u], dd_r.at[s, b, d, u], row, 1 - col)
+
+    def mine_copy(b, u):
+        here = total.at[mine, spot(at, b, 0, u), :]
+        return remote(here, here, mine_s.at[b, u], mine_r.at[b, u], row, 1 - col)
+
+    def pk_copy(s, d):
+        return remote(
+            highs.at[s], seen.at[s, d], pk_s.at[s, d], pk_r.at[s, d], targets[d], col
+        )
 
     peak_first.wait()
-    top[...] = jnp.maximum(peak[...], peaks[0])
-    pk_copy(top, 0).start()
+    highs[0] = jnp.maximum(peak[...], top[...])
+    for d in range(2):
+        pk_copy(0, d).start()
     first.wait()
     own[...] = grad[mine] + other[...]
-    for d, u in streams:
-        rs_copy(own.at[spot(place[d], d, u), :], 0, d, u).start()
+    for b, d, u in flows:
+        rs_copy(own.at[spot(place[d] + reach(b, d), b, d, u), :], 0, b, d, u).start()
+
+    def pass_on(s, b, d, u):
+        inbox[s, box(b, d, u), :] += own[spot(place[d] + reach(b, d) - s - 1, b, d, u), :]
+        rs_copy(inbox.at[s, box(b, d, u), :], s + 1, b, d, u).start()
+
+    def pass_peak(s):
+        for d in range(2):
+            pk_copy(s, d).wait_recv()
+        highs[s + 1] = jnp.maximum(highs[s], jnp.maximum(seen[s, 0], seen[s, 1]))
 
     def scatter_step(s, carry):
-        pk_copy(top, s).wait_recv()
-        peaks[s + 1] = jnp.maximum(peaks[s + 1], top[...])
-        pk_copy(peaks.at[s + 1], s + 1).start()
-        for d, u in streams:
-            rs_copy(own.at[spot(0, d, u), :], s, d, u).wait_recv()
-            inbox[s, box(d, u), :] += own[spot(place[d] - s - 1, d, u), :]
-            rs_copy(inbox.at[s, box(d, u), :], s + 1, d, u).start()
+        pass_peak(s)
+        for d in range(2):
+            pk_copy(s + 1, d).start()
+        for b, d, u in flows:
+            rs_wait(s, b, d, u).wait_recv()
+            pass_on(s, b, d, u)
         return carry
 
-    lax.fori_loop(0, ring - 2, scatter_step, 0)
-    last = ring - 2
-    for d, u in streams:
-        rs_copy(own.at[spot(0, d, u), :], last, d, u).wait_recv()
-        here = spot(place[d] + 1, d, u)
-        total[mine, here, :] = inbox[last, box(d, u), :] + own[here, :]
-        ag_copy(0, d, u).start()
-        dd_copy(0, d, u).start()
-    pk_copy(top, last).wait_recv()
+    lax.fori_loop(0, far - 2, scatter_step, 0)
+    pass_peak(far - 2)
+    for d in range(2):
+        pk_copy(far - 1, d).start()
+    for b, d, u in flows:
+        rs_wait(far - 2, b, d, u).wait_recv()
+        if b == d:
+            pass_on(far - 2, b, d, u)
+    for u in range(len(pieces)):
+        for b in range(2):
+            rs_wait(far - 1, b, b, u).wait_recv()
+            here = spot(at, b, 0, u)
+            total[mine, here, :] = (
+                own[here, :] + inbox[far - 1, box(b, b, u), :] + inbox[far - 2, box(b, 1 - b, u), :]
+            )
+            for d in range(2):
+                ag_copy(0, b, d, u).start()
+            mine_copy(b, u).start()
+    pass_peak(far - 1)
 
     fwd = [
         remote(rims.at[mine, t], rims.at[mine, t], fwd_s.at[t], fwd_r.at[t], row, 1 - col)
@@ -354,29 +518,44 @@
         fwd[0].start()
 
     def gather_step(s, carry):
-        for d, u in streams:
-            ag_copy(s, d, u).wait_recv()
-
-            @pl.when(s < ring - 2)
-            def _():
-                ag_copy(s + 1, d, u).start()
-
-            dd_copy(s + 1, d, u).start()
+        for b, d, u in flows:
+            ag_copy(s, b, d, u).wait_recv()
+            ag_copy(s + 1, b, d, u).start()
+            dd_copy(s, b, d, u).start()
         return carry
 
-    lax.fori_loop(0, ring - 1, gather_step, 0)
+    lax.fori_loop(0, far - 2, gather_step, 0)
+    for b, d, u in flows:
+        ag_copy(far - 2, b, d, u).wait_recv()
+        if b == d:
+            ag_copy(far - 1, b, d, u).start()
+        dd_copy(far - 2, b, d, u).start()
+    for b, d, u in flows:
+        if b == d:
+            ag_copy(far - 1, b, d, u).wait_recv()
+            dd_copy(far - 1, b, d, u).start()
+
+    def settle(s, b, d, u):
+        rs_wait(s, b, d, u).wait_send()
+        ag_copy(s, b, d, u).wait_send()
+        dd_copy(s, b, d, u).wait()
 
     def finish(s, carry):
-        for d, u in streams:
-            rs_copy(own.at[spot(0, d, u), :], s, d, u).wait_send()
-            ag_copy(s, d, u).wait_send()
-            dd_copy(s, d, u).wait()
-        pk_copy(top, s).wait_send()
+        for b, d, u in flows:
+            settle(s, b, d, u)
+        for d in range(2):
+            pk_copy(s, d).wait_send()
         return carry
 
-    lax.fori_loop(0, ring - 1, finish, 0)
-    for d, u in streams:
-        dd_copy(ring - 1, d, u).wait()
+    lax.fori_loop(0, far - 1, finish, 0)
+    for b, d, u in flows:
+        if b == d:
+            settle(far - 1, b, d, u)
+    for d in range(2):
+        pk_copy(far - 1, d).wait_send()
+    for u in range(len(pieces)):
+        for b in range(2):
+            mine_copy(b, u).wait()
     numer_copy.wait()
 
     @pl.when(has_up)
@@ -389,30 +568,31 @@
         down.wait_send()
         fwd[1].wait()
 
-    top[...] = jnp.maximum(peaks[ring - 1], top[...])
-
-
-def object_kernel(places, here, obj, numer, mate, rims, illum, top, out, acc):
+    top[...] = highs[far]
+
+
+def object_kernel(known, obj, numer, mate, rims, illum, top, out, acc):
     tile_rows, tile_cols = illum.shape
     side = numer.shape[2]
     half = side // 2
-    mine = here[0]
+    mine = lax.axis_index("col")
     acc[...] = jnp.zeros_like(acc)
 
-    def put(block, start, k):
-        valid = places[k, 2]
-        block = jnp.where(valid != 0, block, 0.0)
+    def put(block, offset, k):
+        top, left, valid = corner(known, k, tile_rows, tile_cols, half)
+        block = jnp.where(valid > 0.0, block, 0.0)
         rh, rl = split(block[0])
         ih, il = split(block[1])
         stacked = cat([rh, ih, rl, il], 1)
-        picked = dot(row_picker(tile_rows, block.shape[1], start, valid), stacked).astype(BF16)
+        pick = row_picker(tile_rows, block.shape[1], top + offset, valid)
+        picked = dot(pick, stacked).astype(BF16)
         tall = cat([picked[:, i * side : (i + 1) * side] for i in range(4)], 0)
-        acc[...] += dot(tall, col_picker(side, tile_cols, places[k, 1]))
+        acc[...] += dot(tall, col_picker(side, tile_cols, left))
 
     for c in range(2):
-        put(jnp.where(mine == c, numer[...], mate[...]), places[2 + c, 0], 2 + c)
-        put(rims[c, 0], places[c, 0] + half, c)
-        put(rims[c, 1], places[4 + c, 0], 4 + c)
+        put(jnp.where(mine == c, numer[...], mate[...]), 0, 2 + c)
+        put(rims[c, 0], half, c)
+        put(rims[c, 1], 0, 4 + c)
     scale = 1.0 / (illum[...] + 0.1 * jnp.max(top[...]))
     for t in range(2):
         high = acc[t * tile_rows : (t + 1) * tile_rows]
@@ -447,20 +627,24 @@
     modes, side = probe_modes.shape[1:3]
     margin = side // 2
     ring, cores = lax.axis_size("row"), lax.axis_size("col")
-    row, col = lax.axis_index("row"), lax.axis_index("col")
-    origin = jnp.stack([row * tile_rows, col * tile_cols]).astype(jnp.int32)
-
-    extended = padded(obj_field, (("row", 1), ("col", 2)), margin)
-    near = padded(centers.reshape(1, 1, 2), (("row", 0),), 1)
-    mate_list = lax.ppermute(near, "col", [(0, 1), (1, 0)])
-    listed = jnp.where(
-        col == 0, jnp.concatenate([near, mate_list], 1), jnp.concatenate([mate_list, near], 1)
-    ).reshape(3 * cores, 2)
-    steps = jnp.arange(3 * cores, dtype=jnp.int32) // cores - 1 + row
-    valid = ((steps >= 0) & (steps < ring)).astype(jnp.int32)
-    places = jnp.concatenate([listed - margin - origin, valid[:, None]], 1)
-    start = centers[0] - origin
-    window = lax.dynamic_slice(extended, (0, start[0], start[1]), (2, side, side))
+    dma = pltpu.SemaphoreType.DMA
+    marks = jnp.broadcast_to(jnp.tile(centers[0], 4)[:, None], (8, 128))
+    column, known = pl.pallas_call(
+        functools.partial(gather_kernel, ring),
+        out_shape=(struct((2, 3 * tile_rows, side)), struct((3, cores, 8, 128), jnp.int32)),
+        in_specs=[VMEM, VMEM],
+        out_specs=(VMEM, VMEM),
+        scratch_shapes=[
+            pltpu.VMEM((2, tile_rows, cores * tile_cols + side), F32),
+            pltpu.VMEM((2, 2, tile_rows, side), F32),
+            dma((3,)), dma((3,)), dma, dma, dma((2,)), dma((2,)), dma((2,)), dma((2,)),
+        ],
+        compiler_params=pltpu.CompilerParams(
+            vmem_limit_bytes=LIMIT, collective_id=2, has_side_effects=True
+        ),
+        name="gather",
+    )(marks, obj_field)
+    known = known.reshape(3 * cores, 8, 128)
 
     lines = (2 * modes + 1) * margin
     chunk, pieces = ring_split(lines, ring)
@@ -475,17 +659,17 @@
             struct((tile_rows, tile_cols)),
             struct((8, 128)),
         ),
-        in_specs=[SMEM] + [VMEM] * 8,
+        in_specs=[SMEM] + [VMEM] * 9,
         out_specs=(VMEM,) * 4,
         scratch_shapes=[
             pltpu.VMEM((2, modes, side, side), F32),
             pltpu.VMEM((2, side, side), F32),
+            pltpu.VMEM((2, side, side), F32),
         ],
         compiler_params=params,
         name="update",
-    )(places, window, probe_modes, amplitudes[0], *tables(side))
-
-    dma = pltpu.SemaphoreType.DMA
+    )(centers, known, column, probe_modes, amplitudes[0], *tables(side))
+
     total, rims, mate, top = pl.pallas_call(
         functools.partial(exchange_kernel, ring, chunk, pieces),
         out_shape=(
@@ -498,15 +682,15 @@
         out_specs=(VMEM,) * 4,
         scratch_shapes=[
             pltpu.VMEM((depth, side), F32),
-            pltpu.VMEM((ring - 1, 2 * chunk, side), F32),
+            pltpu.VMEM((ring // 2, 4 * chunk, side), F32),
             pltpu.VMEM((depth, side), F32),
-            pltpu.VMEM((ring, 8, 128), F32),
-            dma((2,)), dma((2,)),
-            dma((ring - 1, 2, count)), dma((ring - 1, 2, count)),
-            dma((ring - 1, 2, count)), dma((ring - 1, 2, count)),
-            dma((ring, 2, count)), dma((ring, 2, count)),
+            pltpu.VMEM((ring // 2, 2, 8, 128), F32),
+            pltpu.VMEM((ring // 2 + 1, 8, 128), F32),
+            dma((3,)), dma((3,)),
+            *[dma((ring // 2, 2, 2, count))] * 6,
+            dma((2, count)), dma((2, count)),
             dma((2,)), dma((2,)), dma((2,)), dma((2,)),
-            dma((ring,)), dma((ring,)),
+            dma((ring // 2, 2)), dma((ring // 2, 2)),
         ],
         compiler_params=pltpu.CompilerParams(
             vmem_limit_bytes=LIMIT, collective_id=1, has_side_effects=True
@@ -517,12 +701,12 @@
     new_object = pl.pallas_call(
         object_kernel,
         out_shape=struct(obj_field.shape),
-        in_specs=[SMEM, SMEM] + [VMEM] * 6,
+        in_specs=[VMEM] * 7,
         out_specs=VMEM,
         scratch_shapes=[pltpu.VMEM((4 * tile_rows, tile_cols), F32)],
         compiler_params=params,
         name="object",
-    )(places, col.reshape(1).astype(jnp.int32), obj_field, numer, mate, rims, illum, top)
+    )(known, obj_field, numer, mate, rims, illum, top)
     new_probe = pl.pallas_call(
         probe_kernel,
         out_shape=struct(probe_modes.shape),

time: 141 us -> 111 us (0.79)
  starting transfers between devices: 17.9 us -> 0 us
  waiting for transfers between devices: 16.2 us -> 0 us
  Pallas kernels: 95.7 us -> 107 us
  between operations: 4.66 us -> 0.65 us
  other arithmetic: 2.78 us -> 0 us
    pallas_call x0 -> x1, Pallas kernels: none -> 19.4 us  [local(): pl.pallas_call(functools.partial(gather_kernel, ring), out_shape=(struct(...]
    ppermute x7 -> x0, starting transfers between devices: 17.9 us -> none  [the longest x3 14.1 us: padded(): lax.ppermute(lax.slice_in_dim(block, block.shape[dim] - width, None, axis...]
    ppermute x7 -> x0, waiting for transfers between devices: 16.2 us -> none  [the longest x3 16.2 us: padded(): lax.ppermute(lax.slice_in_dim(block, block.shape[dim] - width, None, axis...]
    pallas_call x1, Pallas kernels: 66.5 us -> 57.8 us  [local(): pl.pallas_call(functools.partial(exchange_kernel, ring, chunk, pieces), o...]
    concatenate x3 -> x0, other arithmetic: 1.95 us -> none  [the longest x2 1.29 us: padded(): block = jnp.concatenate([low, block, high], axis=dim)]
  transfers between devices with their start and end apart: 7 -> 0, of which waited for: 2 -> 0; matrix products, arithmetic and copies ran while one was open for 2% -> 0% of each run, Pallas kernels for 0% -> 0%
where the time goes in v1:
time: 111 us
  Pallas kernels  107 us (96%)
  local copies, waits for them, and re-layouts  2.89 us (3%)
    pallas_call x1, Pallas kernels, local(): pl.pallas_call(functools.partial(exchange_kernel, ring, chunk, pieces), o...  57.8 us
    pallas_call x1, Pallas kernels, local(): pl.pallas_call(update_kernel, out_shape=(struct((2, depth, side)), struct...  20.7 us
    pallas_call x1, Pallas kernels, local(): pl.pallas_call(functools.partial(gather_kernel, ring), out_shape=(struct(...  19.4 us
    pallas_call x1, Pallas kernels, local(): pl.pallas_call(probe_kernel, out_shape=struct(probe_modes.shape), in_spec...  4.68 us
    pallas_call x1, Pallas kernels, local(): pl.pallas_call(object_kernel, out_shape=struct(obj_field.shape), in_specs...  4.53 us

profile of v1, /device:TPU:0, one launch (start us, length us, event | category | flops | bytes accessed | tf_op | source)
XLA Modules:
  0.0 110.7 jit_solution(17080608567632903696)
XLA Ops:
  0.6 0.7 tile.8
  1.3 0.1 broadcast_in_dim.7
  1.4 0.7 broadcast_in_dim.8.marks
  2.0 19.4 %gather.1 = (f32[2,384,256]{2,1,0:T(8,128)}, s32[3,2,8,128]{3,2,1,0:T(8,128)}) custom-call(s32[8,128]{1,0:T(8,128)} %broadcast_in_dim.8.marks, f32[2,128,512]{2,1,0:T(8,128)} %obj.3), custom_call_target="tpu_custom_call" | custom-call | tf_op jit(solution)/shard_map/gather/pallas_call | solution.py:632
  21.4 1.5 %jit_solution_.3.rows_ref = f32[2,128,256]{2,1,0:T(8,128)} broadcast(f32[2,128]{1,0:T(2,128)} %constant.10.clone.lanes_ref), dimensions={0,1} | broadcast | bytes 263168 | tf_op jit(solution)
  22.9 20.7 %update.1 = (f32[2,1664,256]{2,1,0:T(8,128)}, f32[2,256,256]{2,1,0:T(8,128)}, f32[128,512]{1,0:T(8,128)}, f32[8,128]{1,0:T(8,128)}) custom-call(s32[1,2]{1,0:T(1,128)} %center.1, s32[6,8,128]{2,1,0:T(8,128)} %bitcast.4, f32[2,384,256]{2,1,0:T(8,128)} %get-tuple-element.13.column, bf16[2,6,256,256]{3,2,1,0:T(8,128)(2,1)} %probe.5, f32[256,256]{1,0:T(8,128)} %bitcast.3, ...), custom_call_target="tpu_custom_call" | custom-call | tf_op jit(solution)/shard_map/update/pallas_call | solution.py:654
  43.6 57.8 %exchange.1 = (f32[2,1664,256]{2,1,0:T(8,128)}, f32[2,2,2,128,256]{4,3,2,1,0:T(8,128)}, f32[2,256,256]{2,1,0:T(8,128)}, f32[8,128]{1,0:T(8,128)}) custom-call(f32[2,1664,256]{2,1,0:T(8,128)} %get-tuple-element.15.grad, f32[2,256,256]{2,1,0:T(8,128)} %get-tuple-element.14.numer, f32[8,128]{1,0:T(8,128)} %get-tuple-element.16.peak), custom_call_target="tpu_custom_call" | custom-call | tf_op jit(solution)/shard_map/exchange/pallas_call | solution.py:673
  101.5 4.5 %object.1 = f32[2,128,512]{2,1,0:T(8,128)} custom-call(s32[6,8,128]{2,1,0:T(8,128)} %bitcast.5, f32[2,128,512]{2,1,0:T(8,128)} %obj.3, f32[2,256,256]{2,1,0:T(8,128)} %get-tuple-element.14.numer, f32[2,256,256]{2,1,0:T(8,128)} %get-tuple-element.17.mate, f32[2,2,2,128,256]{4,3,2,1,0:T(8,128)} %get-tuple-element.18.rims, f32[128,512]{1,0:T(8,128)} %get-tuple-element.19.illum, ...), custom_call_target="tpu_custom_call" | custom-call | tf_op jit(solution)/shard_map/object/pallas_call | solution.py:701
  106.0 4.7 %probe.4 = f32[2,6,256,256]{3,2,1,0:T(8,128)} custom-call(bf16[2,6,256,256]{3,2,1,0:T(8,128)(2,1)} %probe.5, f32[2,1664,256]{2,1,0:T(8,128)} %get-tuple-element.21.total), custom_call_target="tpu_custom_call" | custom-call | tf_op jit(solution)/shard_map/probe/pallas_call | solution.py:710

commit v2 on v1

--- a/solution.py
+++ b/solution.py
@@ -14,7 +14,7 @@
 BF16 = jnp.bfloat16
 VMEM = pl.BlockSpec(memory_space=pltpu.VMEM)
 SMEM = pl.BlockSpec(memory_space=pltpu.SMEM)
-LIMIT = 60 * 1024 * 1024
+LIMIT = 26 * 1024 * 1024
 
 
 def split(x):
@@ -39,7 +39,7 @@
     matrix = np.block([[cosine, sine], [-sine, cosine]]).astype(np.float32)
     turn = k * (2.0 * math.pi / side)
     lanes = np.stack([np.cos(turn), np.sin(turn)]).astype(np.float32)
-    rows = np.broadcast_to(lanes[:, :, None], (2, half, side))
+    rows = np.ascontiguousarray(np.broadcast_to(lanes[:, :, None], (2, half, side)))
     order = np.concatenate([np.arange(0, side, 2), np.arange(1, side, 2)])
     shuffle = (np.arange(side)[:, None] == order[None, :]).astype(np.float32)
     high = matrix.astype(BF16)
@@ -628,7 +628,8 @@
     margin = side // 2
     ring, cores = lax.axis_size("row"), lax.axis_size("col")
     dma = pltpu.SemaphoreType.DMA
-    marks = jnp.broadcast_to(jnp.tile(centers[0], 4)[:, None], (8, 128))
+    lines_at = lax.broadcasted_iota(jnp.int32, (8, 128), 0)
+    marks = jnp.where(lines_at == 0, centers[0, 0], centers[0, 1])
     column, known = pl.pallas_call(
         functools.partial(gather_kernel, ring),
         out_shape=(struct((2, 3 * tile_rows, side)), struct((3, cores, 8, 128), jnp.int32)),

time: 111 us -> 105 us (0.946)
  Pallas kernels: 107 us -> 93.2 us
  local copies, waits for them, and re-layouts: 2.89 us -> 9.92 us
  other arithmetic: 0 us -> 1.29 us
    unnamed x0 -> x22, local copies, waits for them, and re-layouts: none -> 8.54 us
    pallas_call x1, Pallas kernels: 57.8 us -> 53.5 us  [local(): pl.pallas_call(functools.partial(exchange_kernel, ring, chunk, pieces), o...]
    pallas_call x1, Pallas kernels: 20.7 us -> 17.2 us  [local(): pl.pallas_call(update_kernel, out_shape=(struct((2, depth, side)), struct...]
    pallas_call x1, Pallas kernels: 4.68 us -> 2.29 us  [local(): pl.pallas_call(probe_kernel, out_shape=struct(probe_modes.shape), in_spec...]
    another operation x2 -> x0, local copies, waits for them, and re-layouts: 2.14 us -> none
    pallas_call x1, Pallas kernels: 19.4 us -> 17.4 us  [local(): pl.pallas_call(functools.partial(gather_kernel, ring), out_shape=(struct(...]
    pallas_call x1, Pallas kernels: 4.53 us -> 2.75 us  [local(): pl.pallas_call(object_kernel, out_shape=struct(obj_field.shape), in_specs...]
    slice x0 -> x1, local copies, waits for them, and re-layouts: none -> 1.31 us  [local(): marks = jnp.where(lines_at == 0, centers[0, 0], centers[0, 1])]
where the time goes in v2:
time: 105 us
  Pallas kernels  93.2 us (89%)
  local copies, waits for them, and re-layouts  9.92 us (9%)
  other arithmetic  1.29 us (1%)
    pallas_call x1, Pallas kernels, local(): pl.pallas_call(functools.partial(exchange_kernel, ring, chunk, pieces), o...  53.5 us
    pallas_call x1, Pallas kernels, local(): pl.pallas_call(functools.partial(gather_kernel, ring), out_shape=(struct(...  17.4 us
    pallas_call x1, Pallas kernels, local(): pl.pallas_call(update_kernel, out_shape=(struct((2, depth, side)), struct...  17.2 us
    unnamed x22, local copies, waits for them, and re-layouts  8.54 us
    pallas_call x1, Pallas kernels, local(): pl.pallas_call(object_kernel, out_shape=struct(obj_field.shape), in_specs...  2.75 us
    pallas_call x1, Pallas kernels, local(): pl.pallas_call(probe_kernel, out_shape=struct(probe_modes.shape), in_spec...  2.29 us

profile of v2, /device:TPU:0, one launch (start us, length us, event | category | flops | bytes accessed | tf_op | source)
XLA Modules:
  0.0 105.1 jit_solution(11802875334294180325)
XLA Ops:
  0.6 1.3 %fusion = (s32[1,1]{1,0:T(1,128)}, s32[1,1]{1,0:T(1,128)}) fusion(s32[1,2]{1,0:T(1,128)} %center.1), kind=kLoop, calls=%fused_computation.1 | loop fusion | bytes 16 | tf_op jit(solution)/shard_map/slice | solution.py:632
  1.9 1.3 %compare_select_fusion = s32[8]{0:T(128)S(1)} fusion(s32[]{:T(128)} %bitcast.1, s32[]{:T(128)} %bitcast), kind=kLoop, calls=%fused_computation | loop fusion | flops 16 | bytes 40 | tf_op jit(solution)/shard_map/jit(_where)/select_n | solution.py:632
  3.2 0.1 iota.7.marks
  3.3 0.0 copy-start.2
  3.3 1.0 copy-done.2
  4.4 17.4 %gather.1 = (f32[2,384,256]{2,1,0:T(8,128)S(1)}, s32[3,2,8,128]{3,2,1,0:T(8,128)S(1)}) custom-call(s32[8,128]{1,0:T(8,128)S(1)} %iota.7.marks, f32[2,128,512]{2,1,0:T(8,128)S(1)} %copy-done.2), custom_call_target="tpu_custom_call" | custom-call | tf_op jit(solution)/shard_map/gather/pallas_call | solution.py:633
  21.8 0.0 copy-start
  21.8 1.4 %copy-done = bf16[2,6,256,256]{3,2,1,0:T(8,128)(2,1)S(1)} copy-done((bf16[2,6,256,256]{3,2,1,0:T(8,128)(2,1)S(1)}, bf16[2,6,256,256]{3,2,1,0:T(8,128)(2,1)}, u32[]{:S(2)}) %copy-start) | copy-done | bytes 1572888
  23.2 0.0 copy-start.4
  23.2 0.9 copy-done.4
  24.2 0.0 copy-start.5
  24.2 0.9 copy-done.5
  25.1 0.9 copy-done.6
  26.1 0.9 copy-done.7
  27.0 0.9 copy-done.8
  28.0 0.7 copy-done.9
  28.6 0.7 copy-done.10
  29.3 17.2 %update.1 = (f32[2,1664,256]{2,1,0:T(8,128)S(1)}, f32[2,256,256]{2,1,0:T(8,128)S(1)}, f32[128,512]{1,0:T(8,128)S(1)}, f32[8,128]{1,0:T(8,128)S(1)}) custom-call(s32[1,2]{1,0:T(1,128)S(1)} %copy-done.9, s32[6,8,128]{2,1,0:T(8,128)S(1)} %bitcast.5, f32[2,384,256]{2,1,0:T(8,128)S(1)} %get-tuple-element.13.column, bf16[2,6,256,256]{3,2,1,0:T(8,128)(2,1)S(1)} %copy-done, ...), custom_call_target="tpu_custom_call" | custom-call | tf_op jit(solution)/shard_map/update/pallas_call | solution.py:655
  46.5 0.0 copy-start.1
  46.5 53.5 %exchange.1 = (f32[2,1664,256]{2,1,0:T(8,128)S(1)}, f32[2,2,2,128,256]{4,3,2,1,0:T(8,128)S(1)}, f32[2,256,256]{2,1,0:T(8,128)S(1)}, f32[8,128]{1,0:T(8,128)S(1)}) custom-call(f32[2,1664,256]{2,1,0:T(8,128)S(1)} %get-tuple-element.15.grad, f32[2,256,256]{2,1,0:T(8,128)S(1)} %get-tuple-element.14.numer, f32[8,128]{1,0:T(8,128)S(1)} %get-tuple-element.16.peak), custom_call_target="tpu_custom_call" | custom-call | tf_op jit(solution)/shard_map/exchange/pallas_call | solution.py:674
  100.0 0.0 copy-done.3
  100.0 2.7 %object.1 = f32[2,128,512]{2,1,0:T(8,128)} custom-call(s32[6,8,128]{2,1,0:T(8,128)S(1)} %bitcast.6, f32[2,128,512]{2,1,0:T(8,128)S(1)} %copy-done.3, f32[2,256,256]{2,1,0:T(8,128)S(1)} %get-tuple-element.14.numer, f32[2,256,256]{2,1,0:T(8,128)S(1)} %get-tuple-element.17.mate, f32[2,2,2,128,256]{4,3,2,1,0:T(8,128)S(1)} %get-tuple-element.18.rims, ...), custom_call_target="tpu_custom_call" | custom-call | tf_op jit(solution)/shard_map/object/pallas_call | solution.py:702
  102.8 0.0 copy-done.1
  102.8 2.3 %probe.4 = f32[2,6,256,256]{3,2,1,0:T(8,128)} custom-call(bf16[2,6,256,256]{3,2,1,0:T(8,128)(2,1)S(1)} %copy-done.1, f32[2,1664,256]{2,1,0:T(8,128)S(1)} %get-tuple-element.21.total), custom_call_target="tpu_custom_call" | custom-call | tf_op jit(solution)/shard_map/probe/pallas_call | solution.py:711
  (6 shorter events, 0.0 us)
Async XLA Ops:
  3.3 1.0 copy-start.2
  21.8 1.4 %copy-start = (bf16[2,6,256,256]{3,2,1,0:T(8,128)(2,1)S(1)}, bf16[2,6,256,256]{3,2,1,0:T(8,128)(2,1)}, u32[]{:S(2)}) copy-start(bf16[2,6,256,256]{3,2,1,0:T(8,128)(2,1)} %probe.5) | copy-start | bytes 4718596
  23.2 0.9 copy-start.4
  24.2 0.9 copy-start.5
  25.1 0.9 copy-start.6
  26.1 0.9 copy-start.7
  27.0 0.9 copy-start.8
  28.0 0.7 copy-start.9
  28.6 0.7 copy-start.10
  29.3 70.7 %copy-start.3 = (f32[2,128,512]{2,1,0:T(8,128)S(1)}, f32[2,128,512]{2,1,0:T(8,128)}, u32[]{:S(2)}) copy-start(f32[2,128,512]{2,1,0:T(8,128)} %obj.3) | copy-start | bytes 1572868
  46.5 56.3 %copy-start.1 = (bf16[2,6,256,256]{3,2,1,0:T(8,128)(2,1)S(1)}, bf16[2,6,256,256]{3,2,1,0:T(8,128)(2,1)}, u32[]{:S(2)}) copy-start(bf16[2,6,256,256]{3,2,1,0:T(8,128)(2,1)} %probe.5) | copy-start | bytes 4718596

commit v3 on v2

--- a/solution.py
+++ b/solution.py
@@ -107,11 +107,10 @@
     return jnp.where(place == start, 1.0, 0.0).astype(BF16)
 
 
-def corner(known, k, tile_rows, tile_cols, margin):
+def corner(mark, k, tile_rows, tile_cols, margin):
     row, col = lax.axis_index("row"), lax.axis_index("col")
     line = row + k // 2 - 1
     inside = (line >= 0) & (line < lax.axis_size("row"))
-    mark = known[k]
     return (
         mark[0:1, 0:1] - (row * tile_rows + margin),
         mark[1:2, 0:1] - (col * tile_cols + margin),
@@ -120,8 +119,8 @@
 
 
 def update_kernel(
-    center, known, column, probe, amp, a_ref, b_ref, rows_ref, lanes_ref, shuffle,
-    grad, numer, illum, peak, far, power, window,
+    center, column, probe, amp, a_ref, b_ref, rows_ref, lanes_ref,
+    grad, numer, far, power, window,
 ):
     modes, side = probe.shape[1], probe.shape[2]
     half = side // 2
@@ -135,7 +134,7 @@
         wr, wi = window[0], window[1]
         return pr, pi, wr, wi, pr * wr - pi * wi, pr * wi + pi * wr
 
-    start = center[0, 0] - lax.axis_index("row") * illum.shape[0]
+    start = center[0, 0] - lax.axis_index("row") * (column.shape[1] // 3)
     base = pl.multiple_of(start // 8 * 8, 8)
     shift = lax.rem(side + 8 - lax.rem(start, 8), side + 8)
     for i in range(2):
@@ -147,38 +146,16 @@
         fr, fi = forward_transform(xr, xi, a, b, rows, lanes)
         far[0, m] = fr
         far[1, m] = fi
-        power[0] += fr * fr + fi * fi
-        power[1] += pr * pr + pi * pi
+        power[...] += fr * fr + fi * fi
         return carry
 
     lax.fori_loop(0, modes, ahead, 0)
-    measured = 0.0
-    rest = amp[...]
-    for i in range(3):
-        piece = rest.astype(BF16)
-        rest = rest - piece.astype(F32)
-        measured += dot(dot(shuffle[1], piece).astype(BF16), shuffle[0])
-    power[0] = measured / (jnp.sqrt(power[0]) + 0.5)
-    high, low = split(power[1])
-    tile_rows, tile_cols = illum.shape
-    spot = cat([high, low], 1)
-    illum[...] = jnp.zeros_like(illum)
-
-    def place_spot(k, carry):
-        top, left, valid = corner(known, k, tile_rows, tile_cols, half)
-        picked = dot(row_picker(tile_rows, side, top, valid), spot).astype(BF16)
-        across = col_picker(side, tile_cols, left)
-        placed = dot(cat([picked[:, :side], picked[:, side:]], 0), across)
-        illum[...] += placed[:tile_rows] + placed[tile_rows:]
-        return carry
-
-    lax.fori_loop(0, known.shape[0], place_spot, 0)
-    peak[...] = jnp.full(peak.shape, jnp.max(illum[...]), F32)
+    power[...] = amp[...] / (jnp.sqrt(power[...]) + 0.5)
     numer[...] = jnp.zeros_like(numer)
 
     def back(m, carry):
         pr, pi, wr, wi, xr, xi = wave(m)
-        factor = power[0]
+        factor = power[...]
         gr, gi = inverse_transform(far[0, m] * factor, far[1, m] * factor, a, b, rows, lanes)
         dr, di = gr - xr, gi - xi
         numer[0] += pr * dr + pi * di
@@ -202,9 +179,18 @@
 
 
 def gather_kernel(
-    ring, marks, obj, column, known,
+    ring, marks, obj, probe_hbm, amp_hbm, shuffle_hbm, column, known, measured, illum, peak,
     strip, packed, near_s, near_r, tile_s, tile_r, pack_s, pack_r, pass_s, pass_r,
+    probe, amp, shuffle, load_s,
 ):
+    loads = [
+        pltpu.make_async_copy(src, dst, load_s.at[i])
+        for i, (src, dst) in enumerate(
+            ((probe_hbm, probe), (amp_hbm, amp), (shuffle_hbm, shuffle))
+        )
+    ]
+    for load in loads:
+        load.start()
     row, col = lax.axis_index("row"), lax.axis_index("col")
     tile_rows, tile_cols = obj.shape[1:]
     side = column.shape[2]
@@ -305,12 +291,35 @@
                 (2, tile_rows, side), F32
             )
 
+    for load in loads:
+        load.wait()
+    found, rest = 0.0, amp[...]
+    for i in range(3):
+        piece = rest.astype(BF16)
+        rest = rest - piece.astype(F32)
+        found += dot(dot(shuffle[1], piece).astype(BF16), shuffle[0])
+    measured[...] = found
+    spot = 0.0
+    for m in range(probe.shape[1]):
+        pr, pi = probe[0, m].astype(F32), probe[1, m].astype(F32)
+        spot += pr * pr + pi * pi
+    spot = cat(split(spot), 1)
     mate_mark.wait()
     for t in range(2):
 
         @pl.when(has[t])
         def _():
             share(t).wait()
+
+    total = 0.0
+    for k in range(6):
+        top, left, valid = corner(known[k // 2, k % 2], k, tile_rows, tile_cols, half)
+        picked = dot(row_picker(tile_rows, side, top, valid), spot).astype(BF16)
+        tall = cat([picked[:, :side], picked[:, side:]], 0)
+        placed = dot(tall, col_picker(side, tile_cols, left))
+        total += placed[:tile_rows] + placed[tile_rows:]
+    illum[...] = total
+    peak[...] = jnp.full(peak.shape, jnp.max(total), F32)
 
     for t in range(2):
 
@@ -335,7 +344,8 @@
 
 
 def exchange_kernel(
-    ring, chunk, pieces, grad, numer, peak, total, rims, mate, top,
+    ring, chunk, pieces, known, grad, numer, peak, total, acc, top,
+    rims, mate,
     own, inbox, other, seen, highs, core_s, core_r, rs_s, rs_r, ag_s, ag_r, dd_s, dd_r,
     mine_s, mine_r, rim_s, rim_r, fwd_s, fwd_r, pk_s, pk_r,
 ):
@@ -530,6 +540,32 @@
         if b == d:
             ag_copy(far - 1, b, d, u).start()
         dd_copy(far - 2, b, d, u).start()
+    tile_rows, tile_cols = acc.shape[0] // 4, acc.shape[1]
+
+    def put(block, offset, k):
+        top, left, valid = corner(known[k], k, tile_rows, tile_cols, half)
+        block = jnp.where(valid > 0.0, block, 0.0)
+        rh, rl = split(block[0])
+        ih, il = split(block[1])
+        stacked = cat([rh, ih, rl, il], 1)
+        pick = row_picker(tile_rows, block.shape[1], top + offset, valid)
+        picked = dot(pick, stacked).astype(BF16)
+        tall = cat([picked[:, i * side : (i + 1) * side] for i in range(4)], 0)
+        acc[...] += dot(tall, col_picker(side, tile_cols, left))
+
+    numer_copy.wait()
+    for t in range(2):
+
+        @pl.when((has_up, has_down)[t])
+        def _():
+            fwd[t].wait()
+
+    acc[...] = jnp.zeros_like(acc)
+    for c in range(2):
+        put(jnp.where(mine == c, numer[...], mate[...]), 0, 2 + c)
+        put(rims[c, 0], half, c)
+        put(rims[c, 1], 0, 4 + c)
+
     for b, d, u in flows:
         if b == d:
             ag_copy(far - 1, b, d, u).wait_recv()
@@ -556,43 +592,20 @@
     for u in range(len(pieces)):
         for b in range(2):
             mine_copy(b, u).wait()
-    numer_copy.wait()
 
     @pl.when(has_up)
     def _():
         up.wait_send()
-        fwd[0].wait()
 
     @pl.when(has_down)
     def _():
         down.wait_send()
-        fwd[1].wait()
 
     top[...] = highs[far]
 
 
-def object_kernel(known, obj, numer, mate, rims, illum, top, out, acc):
-    tile_rows, tile_cols = illum.shape
-    side = numer.shape[2]
-    half = side // 2
-    mine = lax.axis_index("col")
-    acc[...] = jnp.zeros_like(acc)
-
-    def put(block, offset, k):
-        top, left, valid = corner(known, k, tile_rows, tile_cols, half)
-        block = jnp.where(valid > 0.0, block, 0.0)
-        rh, rl = split(block[0])
-        ih, il = split(block[1])
-        stacked = cat([rh, ih, rl, il], 1)
-        pick = row_picker(tile_rows, block.shape[1], top + offset, valid)
-        picked = dot(pick, stacked).astype(BF16)
-        tall = cat([picked[:, i * side : (i + 1) * side] for i in range(4)], 0)
-        acc[...] += dot(tall, col_picker(side, tile_cols, left))
-
-    for c in range(2):
-        put(jnp.where(mine == c, numer[...], mate[...]), 0, 2 + c)
-        put(rims[c, 0], half, c)
-        put(rims[c, 1], 0, 4 + c)
+def object_kernel(obj, acc, illum, top, out):
+    tile_rows = illum.shape[0]
     scale = 1.0 / (illum[...] + 0.1 * jnp.max(top[...]))
     for t in range(2):
         high = acc[t * tile_rows : (t + 1) * tile_rows]
@@ -630,21 +643,35 @@
     dma = pltpu.SemaphoreType.DMA
     lines_at = lax.broadcasted_iota(jnp.int32, (8, 128), 0)
     marks = jnp.where(lines_at == 0, centers[0, 0], centers[0, 1])
-    column, known = pl.pallas_call(
+    *consts, shuffle = tables(side)
+    column, known, measured, illum, peak = pl.pallas_call(
         functools.partial(gather_kernel, ring),
-        out_shape=(struct((2, 3 * tile_rows, side)), struct((3, cores, 8, 128), jnp.int32)),
-        in_specs=[VMEM, VMEM],
-        out_specs=(VMEM, VMEM),
+        out_shape=(
+            struct((2, 3 * tile_rows, side)),
+            struct((3, cores, 8, 128), jnp.int32),
+            struct((side, side)),
+            struct((tile_rows, tile_cols)),
+            struct((8, 128)),
+        ),
+        in_specs=[VMEM] * 2 + [pl.BlockSpec(memory_space=pltpu.HBM)] * 3,
+        out_specs=(VMEM,) * 5,
         scratch_shapes=[
             pltpu.VMEM((2, tile_rows, cores * tile_cols + side), F32),
             pltpu.VMEM((2, 2, tile_rows, side), F32),
             dma((3,)), dma((3,)), dma, dma, dma((2,)), dma((2,)), dma((2,)), dma((2,)),
+            pltpu.VMEM(probe_modes.shape, BF16),
+            pltpu.VMEM((side, side), F32),
+            pltpu.VMEM((2, side, side), BF16),
+            dma((3,)),
         ],
         compiler_params=pltpu.CompilerParams(
             vmem_limit_bytes=LIMIT, collective_id=2, has_side_effects=True
         ),
+        cost_estimate=pl.CostEstimate(
+            flops=4 * 10**9, bytes_accessed=40 * 10**6, transcendentals=0
+        ),
         name="gather",
-    )(marks, obj_field)
+    )(marks, obj_field, probe_modes, amplitudes[0], shuffle)
     known = known.reshape(3 * cores, 8, 128)
 
     lines = (2 * modes + 1) * margin
@@ -652,36 +679,35 @@
     depth = 2 * ring * chunk
     count = len(pieces)
     params = pltpu.CompilerParams(vmem_limit_bytes=LIMIT)
-    grad, numer, illum, peak = pl.pallas_call(
+    grad, numer = pl.pallas_call(
         update_kernel,
         out_shape=(
             struct((2, depth, side)),
             struct((2, side, side)),
-            struct((tile_rows, tile_cols)),
-            struct((8, 128)),
         ),
-        in_specs=[SMEM] + [VMEM] * 9,
-        out_specs=(VMEM,) * 4,
+        in_specs=[SMEM] + [VMEM] * 7,
+        out_specs=(VMEM,) * 2,
         scratch_shapes=[
             pltpu.VMEM((2, modes, side, side), F32),
-            pltpu.VMEM((2, side, side), F32),
+            pltpu.VMEM((side, side), F32),
             pltpu.VMEM((2, side, side), F32),
         ],
         compiler_params=params,
         name="update",
-    )(centers, known, column, probe_modes, amplitudes[0], *tables(side))
-
-    total, rims, mate, top = pl.pallas_call(
+    )(centers, column, probe_modes, measured, *consts)
+
+    total, acc, top = pl.pallas_call(
         functools.partial(exchange_kernel, ring, chunk, pieces),
         out_shape=(
             struct((2, depth, side)),
-            struct((2, 2, 2, margin, side)),
-            struct((2, side, side)),
+            struct((4 * tile_rows, tile_cols)),
             struct((8, 128)),
         ),
-        in_specs=[VMEM] * 3,
-        out_specs=(VMEM,) * 4,
+        in_specs=[VMEM] * 4,
+        out_specs=(VMEM,) * 3,
         scratch_shapes=[
+            pltpu.VMEM((2, 2, 2, margin, side), F32),
+            pltpu.VMEM((2, side, side), F32),
             pltpu.VMEM((depth, side), F32),
             pltpu.VMEM((ring // 2, 4 * chunk, side), F32),
             pltpu.VMEM((depth, side), F32),
@@ -697,17 +723,16 @@
             vmem_limit_bytes=LIMIT, collective_id=1, has_side_effects=True
         ),
         name="exchange",
-    )(grad, numer, peak)
+    )(known, grad, numer, peak)
 
     new_object = pl.pallas_call(
         object_kernel,
         out_shape=struct(obj_field.shape),
-        in_specs=[VMEM] * 7,
+        in_specs=[VMEM] * 4,
         out_specs=VMEM,
-        scratch_shapes=[pltpu.VMEM((4 * tile_rows, tile_cols), F32)],
         compiler_params=params,
         name="object",
-    )(known, obj_field, numer, mate, rims, illum, top)
+    )(obj_field, acc, illum, top)
     new_probe = pl.pallas_call(
         probe_kernel,
         out_shape=struct(probe_modes.shape),

time: 105 us -> 96.6 us (0.920)
  Pallas kernels: 93.2 us -> 88.5 us
  local copies, waits for them, and re-layouts: 9.92 us -> 5.77 us
    unnamed x22, local copies, waits for them, and re-layouts: 8.54 us -> 4.38 us
    pallas_call x1, Pallas kernels: 17.2 us -> 14 us  [local(): pl.pallas_call(update_kernel, out_shape=(struct((2, depth, side)), struct...]
    pallas_call x1, Pallas kernels: 2.75 us -> 1.03 us  [local(): pl.pallas_call(object_kernel, out_shape=struct(obj_field.shape), in_specs...]
where the time goes in v3:
time: 96.6 us; the launch traced here: 96.3 us
  Pallas kernels  88.5 us (92%)
  local copies, waits for them, and re-layouts  5.77 us (6%)
  other arithmetic  1.29 us (1%)
    pallas_call x1, Pallas kernels, local(): pl.pallas_call(functools.partial(exchange_kernel, ring, chunk, pieces), o...  53.5 us
    pallas_call x1, Pallas kernels, local(): pl.pallas_call(functools.partial(gather_kernel, ring), out_shape=(struct(...  17.7 us
    pallas_call x1, Pallas kernels, local(): pl.pallas_call(update_kernel, out_shape=(struct((2, depth, side)), struct...  14 us
    unnamed x22, local copies, waits for them, and re-layouts  4.38 us
    pallas_call x1, Pallas kernels, local(): pl.pallas_call(probe_kernel, out_shape=struct(probe_modes.shape), in_spec...  2.32 us

profile of v3, /device:TPU:0, one launch (start us, length us, event | category | flops | bytes accessed | tf_op | source)
XLA Modules:
  0.0 96.3 jit_solution(11326933015549275372)
XLA Ops:
  0.6 1.3 %fusion = (s32[1,1]{1,0:T(1,128)}, s32[1,1]{1,0:T(1,128)}) fusion(s32[1,2]{1,0:T(1,128)} %center.1), kind=kLoop, calls=%fused_computation.1 | loop fusion | bytes 16 | tf_op jit(solution)/shard_map/slice | solution.py:645
  1.9 1.3 %compare_select_fusion = s32[8]{0:T(128)S(1)} fusion(s32[]{:T(128)} %bitcast.1, s32[]{:T(128)} %bitcast), kind=kLoop, calls=%fused_computation | loop fusion | flops 16 | bytes 40 | tf_op jit(solution)/shard_map/jit(_where)/select_n | solution.py:645
  3.2 0.1 iota.7.marks
  3.3 0.0 copy-start
  3.3 1.4 %copy-done = bf16[2,6,256,256]{3,2,1,0:T(8,128)(2,1)S(1)} copy-done((bf16[2,6,256,256]{3,2,1,0:T(8,128)(2,1)S(1)}, bf16[2,6,256,256]{3,2,1,0:T(8,128)(2,1)}, u32[]{:S(2)}) %copy-start) | copy-done | bytes 1572888
  4.7 0.0 copy-start.2
  4.7 1.0 %copy-done.2 = f32[2,128,512]{2,1,0:T(8,128)S(1)} copy-done((f32[2,128,512]{2,1,0:T(8,128)S(1)}, f32[2,128,512]{2,1,0:T(8,128)}, u32[]{:S(2)}) %copy-start.2) | copy-done | bytes 524312
  5.8 0.9 copy-done.9
  6.7 0.9 copy-done.10
  7.7 0.0 copy-start.7
  7.7 0.0 copy-start.8
  7.7 17.7 %gather.1 = (f32[2,384,256]{2,1,0:T(8,128)S(1)}, s32[3,2,8,128]{3,2,1,0:T(8,128)S(1)}, f32[256,256]{1,0:T(8,128)S(1)}, f32[128,512]{1,0:T(8,128)S(1)}, f32[8,128]{1,0:T(8,128)S(1)}) custom-call(s32[8,128]{1,0:T(8,128)S(1)} %iota.7.marks, f32[2,128,512]{2,1,0:T(8,128)S(1)} %copy-done.2, bf16[2,6,256,256]{3,2,1,0:T(8,128)(2,1)S(1)} %copy-done, ...), custom_call_target="tpu_custom_call" | custom-call | flops 4000000000 | bytes 40000000 | tf_op jit(solution)/shard_map/gather/pallas_call | solution.py:647
  25.4 0.0 copy-done.1
  25.4 0.0 copy-done.4
  25.4 0.0 copy-done.5
  25.4 0.0 copy-done.6
  25.4 0.0 copy-done.7
  25.4 0.0 copy-done.8
  25.4 0.0 copy-start.3
  25.4 14.0 %update.1 = (f32[2,1664,256]{2,1,0:T(8,128)S(1)}, f32[2,256,256]{2,1,0:T(8,128)S(1)}) custom-call(s32[1,2]{1,0:T(1,128)S(1)} %copy-done.7, f32[2,384,256]{2,1,0:T(8,128)S(1)} %get-tuple-element.13.column, bf16[2,6,256,256]{3,2,1,0:T(8,128)(2,1)S(1)} %copy-done.1, f32[256,256]{1,0:T(8,128)S(1)} %get-tuple-element.14.amp, bf16[2,256,256]{2,1,0:T(8,128)(2,1)S(1)} %copy-done.6, ...), custom_call_target="tpu_custom_call" | custom-call | tf_op jit(solution)/shard_map/update/pallas_call | solution.py:682
  39.5 53.5 %exchange.1 = (f32[2,1664,256]{2,1,0:T(8,128)S(1)}, f32[512,512]{1,0:T(8,128)S(1)}, f32[8,128]{1,0:T(8,128)S(1)}) custom-call(s32[6,8,128]{2,1,0:T(8,128)S(1)} %bitcast.4, f32[2,1664,256]{2,1,0:T(8,128)S(1)} %get-tuple-element.15.grad, f32[2,256,256]{2,1,0:T(8,128)S(1)} %get-tuple-element.16.numer, f32[8,128]{1,0:T(8,128)S(1)} %get-tuple-element.17.peak), custom_call_target="tpu_custom_call" | custom-call | tf_op jit(solution)/shard_map/exchange/pallas_call | solution.py:699
  93.0 0.0 copy-done.3
  93.0 1.0 %object.1 = f32[2,128,512]{2,1,0:T(8,128)} custom-call(f32[2,128,512]{2,1,0:T(8,128)S(1)} %copy-done.3, f32[512,512]{1,0:T(8,128)S(1)} %get-tuple-element.18.acc, f32[128,512]{1,0:T(8,128)S(1)} %get-tuple-element.19.illum, f32[8,128]{1,0:T(8,128)S(1)} %get-tuple-element.20.top), custom_call_target="tpu_custom_call" | custom-call | tf_op jit(solution)/shard_map/object/pallas_call | solution.py:728
  94.0 2.3 %probe.4 = f32[2,6,256,256]{3,2,1,0:T(8,128)} custom-call(bf16[2,6,256,256]{3,2,1,0:T(8,128)(2,1)S(1)} %copy-done.1, f32[2,1664,256]{2,1,0:T(8,128)S(1)} %get-tuple-element.21.total), custom_call_target="tpu_custom_call" | custom-call | tf_op jit(solution)/shard_map/probe/pallas_call | solution.py:736
  (6 shorter events, 0.0 us)
Async XLA Ops:
  3.3 1.4 %copy-start = (bf16[2,6,256,256]{3,2,1,0:T(8,128)(2,1)S(1)}, bf16[2,6,256,256]{3,2,1,0:T(8,128)(2,1)}, u32[]{:S(2)}) copy-start(bf16[2,6,256,256]{3,2,1,0:T(8,128)(2,1)} %probe.5) | copy-start | bytes 4718596
  4.7 1.0 %copy-start.2 = (f32[2,128,512]{2,1,0:T(8,128)S(1)}, f32[2,128,512]{2,1,0:T(8,128)}, u32[]{:S(2)}) copy-start(f32[2,128,512]{2,1,0:T(8,128)} %obj.3) | copy-start | bytes 1572868
  5.8 0.9 copy-start.9
  6.7 0.9 copy-start.10
  7.7 17.7 %copy-start.1 = (bf16[2,6,256,256]{3,2,1,0:T(8,128)(2,1)S(1)}, bf16[2,6,256,256]{3,2,1,0:T(8,128)(2,1)}, u32[]{:S(2)}) copy-start(bf16[2,6,256,256]{3,2,1,0:T(8,128)(2,1)} %probe.5) | copy-start | bytes 4718596
  7.7 17.7 %copy-start.4 = (f32[2,128,256]{2,1,0:T(8,128)S(1)}, f32[2,128,256]{2,1,0:T(8,128)}, u32[]{:S(2)}) copy-start(f32[2,128,256]{2,1,0:T(8,128)} %constant.14.clone.rows_ref) | copy-start | bytes 786436
  7.7 17.7 %copy-start.5 = (bf16[2,256,256]{2,1,0:T(8,128)(2,1)S(1)}, bf16[2,256,256]{2,1,0:T(8,128)(2,1)}, u32[]{:S(2)}) copy-start(bf16[2,256,256]{2,1,0:T(8,128)(2,1)} %constant.13.clone.b_ref) | copy-start | bytes 786436
  7.7 17.7 %copy-start.6 = (bf16[2,256,256]{2,1,0:T(8,128)(2,1)S(1)}, bf16[2,256,256]{2,1,0:T(8,128)(2,1)}, u32[]{:S(2)}) copy-start(bf16[2,256,256]{2,1,0:T(8,128)(2,1)} %constant.12.clone.a_ref) | copy-start | bytes 786436
  7.7 17.7 %copy-start.7 = (s32[1,2]{1,0:T(1,128)S(1)}, s32[1,2]{1,0:T(1,128)}, u32[]{:S(2)}) copy-start(s32[1,2]{1,0:T(1,128)} %center.1) | copy-start | bytes 28
  7.7 17.7 %copy-start.8 = (f32[2,128]{1,0:T(2,128)S(1)}, f32[2,128]{1,0:T(2,128)}, u32[]{:S(2)}) copy-start(f32[2,128]{1,0:T(2,128)} %constant.15.clone.lanes_ref) | copy-start | bytes 3076
  25.4 67.6 %copy-start.3 = (f32[2,128,512]{2,1,0:T(8,128)S(1)}, f32[2,128,512]{2,1,0:T(8,128)}, u32[]{:S(2)}) copy-start(f32[2,128,512]{2,1,0:T(8,128)} %obj.3) | copy-start | bytes 1572868
